TPU v7x, 128 devices: a whole 4x4x4 slice. The times are simulated.
128 devices in a mesh: dev: 128 (over z, x, y, core).
Axes of the slice: x: 4, y: 4, z: 4, core: 2. Of those that a mesh axis runs over, the one named last changes fastest.
Arguments:
- state: float32 [2, 4194304], P(None, 'dev'), as said below
- angles: float32 [22, 3], replicated, may hold values from -3.140625 to 3.140625
- sample_high: int32 [1048576, 1], P('dev'), may hold values from 0 to 127; in each aligned block of 8192 rows (0 to 8191, 8192 to 16383, ...) at most 256 rows name the same one
- sample_low: int32 [1048576], P('dev'), may hold values from 0 to 32767
- marginal_qubits: int32 [10], replicated, may hold values from 0 to 21, as said below
Outputs:
- sample_probs: float32 [1048576], P('dev')
- histogram: float32 [1024], P('dev')
- fidelity: float32 [], replicated
Inputs may be any that keep to these rules, and one draw needn't show every extreme that they name: The state is unit noise times a product over qubits of factors between exp(-0.2) and exp(0.2). `marginal_qubits`: 10 different qubit numbers. `sample_high`: among the rows of one device no value occurs more than 256 times, and in some devices one value occurs exactly 256 times.
All inputs are finite; a program needn't handle non-finite values.
Results may differ from a plain program's by a relative error of at most 0.00075.
Values sent between devices are 32-bit elements.
A program may use at most 64 MiB of HBM per device.

v0:
```python
import jax
import jax.numpy as jnp
from jax import lax
from jax.sharding import Mesh
from jax.sharding import PartitionSpec as P

DEV = ("dev_0", "dev_1", "dev_2", "dev_3")


def one_axis_at_a_time(shard, axes):
    for axis in axes:
        shard = lax.psum(shard, axis)
    return shard


def gate_parts(angles):
    theta = angles[:, 0]
    first = angles[:, 1]
    second = angles[:, 2]
    cosine = jnp.cos(theta)
    sine = jnp.sin(theta)
    zeros = jnp.zeros_like(cosine)
    real_part = jnp.stack(
        [
            jnp.stack([cosine, -jnp.cos(second) * sine], -1),
            jnp.stack([jnp.cos(first) * sine, jnp.cos(first + second) * cosine], -1),
        ],
        -2,
    )
    imag_part = jnp.stack(
        [
            jnp.stack([zeros, -jnp.sin(second) * sine], -1),
            jnp.stack([jnp.sin(first) * sine, jnp.sin(first + second) * cosine], -1),
        ],
        -2,
    )
    return (real_part, imag_part)


def kron_gates(gate_real, gate_imag, chosen):
    mat_real = gate_real[chosen[0]]
    mat_imag = gate_imag[chosen[0]]
    for qubit in chosen[1:]:
        next_real = jnp.kron(mat_real, gate_real[qubit]) - jnp.kron(mat_imag, gate_imag[qubit])
        next_imag = jnp.kron(mat_real, gate_imag[qubit]) + jnp.kron(mat_imag, gate_real[qubit])
        mat_real, mat_imag = (next_real, next_imag)
    return (mat_real, mat_imag)


def apply_block(mat_real, mat_imag, field_real, field_imag):

    def product(matrix, field):
        return jnp.einsum("ij,hjc->hic", matrix, field, precision=lax.Precision.HIGHEST)

    new_real = product(mat_real, field_real) - product(mat_imag, field_imag)
    new_imag = product(mat_real, field_imag) + product(mat_imag, field_real)
    return (new_real, new_imag)


def lookup_rows(weight_rows, offsets):
    lane_count = weight_rows.shape[1]
    lane_bits = lane_count.bit_length() - 1
    lane_ids = jnp.arange(lane_count, dtype=jnp.int32)

    def one_block(block):
        upper = block >> lane_bits
        lower = block & lane_count - 1
        picked = jnp.take(weight_rows, upper, axis=0)
        return jnp.sum(jnp.where(lower[:, None] == lane_ids[None, :], picked, 0.0), axis=1)

    total = offsets.shape[0]
    if total % 1024 == 0 and total > 1024:
        return lax.map(one_block, offsets.reshape(total // 1024, 1024)).reshape(total)
    return one_block(offsets)


def on_device(state, angles, sample_high, sample_low, marginal_qubits):
    devices = lax.axis_size(DEV)
    global_bits = devices.bit_length() - 1
    amps_local = state.shape[1]
    local_bits = amps_local.bit_length() - 1
    qubits = local_bits + global_bits
    position = lax.axis_index(DEV)
    gate_real, gate_imag = gate_parts(angles)
    real_part = state[0]
    imag_part = state[1]
    for first_qubit in range(0, local_bits, 6):
        width = min(6, local_bits - first_qubit)
        chosen = list(range(first_qubit + width - 1, first_qubit - 1, -1))
        mat_real, mat_imag = kron_gates(gate_real, gate_imag, chosen)
        shape = (amps_local // 2 ** (first_qubit + width), 2**width, 2**first_qubit)
        real_part, imag_part = apply_block(
            mat_real, mat_imag, real_part.reshape(shape), imag_part.reshape(shape)
        )
        real_part = real_part.reshape(amps_local)
        imag_part = imag_part.reshape(amps_local)
    stride = amps_local // devices
    stacked = jnp.stack([real_part, imag_part]).reshape(2, devices, stride)
    swapped = lax.all_to_all(stacked, DEV, split_axis=1, concat_axis=1, tiled=True)
    mat_real, mat_imag = kron_gates(
        gate_real, gate_imag, list(range(qubits - 1, local_bits - 1, -1))
    )
    new_real, new_imag = apply_block(mat_real, mat_imag, swapped[0][None], swapped[1][None])
    restored = lax.all_to_all(
        jnp.stack([new_real[0], new_imag[0]]), DEV, split_axis=1, concat_axis=1, tiled=True
    )
    real_part = restored[0].reshape(amps_local)
    imag_part = restored[1].reshape(amps_local)
    weight = real_part * real_part + imag_part * imag_part
    lane_total = min(128, amps_local)
    weight_rows = weight.reshape(amps_local // lane_total, lane_total)
    samp_local = sample_low.shape[0]
    owner = sample_high[:, 0]
    capacity = 4 * samp_local // devices
    block_rows = min(512, samp_local)
    block_count = samp_local // block_rows
    owner_hot = (owner[:, None] == jnp.arange(devices, dtype=jnp.int32)[None, :]).astype(
        jnp.float32
    )
    hot_blocks = owner_hot.reshape(block_count, block_rows, devices).astype(jnp.bfloat16)
    row_ids = jnp.arange(block_rows, dtype=jnp.int32)
    earlier = (row_ids[:, None] > row_ids[None, :]).astype(jnp.bfloat16)
    within = jnp.einsum("ij,bjd->bid", earlier, hot_blocks, preferred_element_type=jnp.float32)
    block_totals = jnp.sum(owner_hot.reshape(block_count, block_rows, devices), axis=1)
    block_before = jnp.cumsum(block_totals, axis=0) - block_totals
    ranking = jnp.sum(
        (within + block_before[:, None, :]) * owner_hot.reshape(block_count, block_rows, devices),
        axis=2,
    ).reshape(samp_local)
    rank_hot = (ranking[:, None] == jnp.arange(capacity, dtype=jnp.float32)[None, :]).astype(
        jnp.float32
    )
    shifted_low = (sample_low + 1).astype(jnp.float32)
    placed = jnp.dot(
        (owner_hot * shifted_low[:, None]).T, rank_hot, precision=lax.Precision.HIGHEST
    )
    requests = placed.astype(jnp.int32) - 1
    incoming = lax.all_to_all(requests, DEV, split_axis=0, concat_axis=0, tiled=True)
    found = lookup_rows(weight_rows, jnp.maximum(incoming, 0).reshape(devices * capacity))
    answers = jnp.where(incoming >= 0, found.reshape(devices, capacity), 0.0)
    replies = lax.all_to_all(answers, DEV, split_axis=0, concat_axis=0, tiled=True)
    values = jnp.sum(
        jnp.dot(owner_hot, replies, precision=lax.Precision.HIGHEST) * rank_hot, axis=1
    )
    marg_count = marginal_qubits.shape[0]
    bin_count = 2**marg_count
    per_device = bin_count // devices
    lower_bits = local_bits // 2
    lower_size = 2**lower_bits
    upper_size = amps_local // lower_size
    places = jnp.arange(marg_count, dtype=jnp.int32)
    is_lower = marginal_qubits < lower_bits
    is_upper = (marginal_qubits >= lower_bits) & (marginal_qubits < local_bits)
    is_global = marginal_qubits >= local_bits
    lower_ids = jnp.arange(lower_size, dtype=jnp.int32)
    upper_ids = jnp.arange(upper_size, dtype=jnp.int32)
    lower_code = jnp.sum(
        jnp.where(
            is_lower[None, :],
            (lower_ids[:, None] >> jnp.minimum(marginal_qubits, 30)[None, :] & 1)
            << places[None, :],
            0,
        ),
        axis=1,
    )
    upper_shift = jnp.clip(marginal_qubits - lower_bits, 0, 30)
    upper_code = jnp.sum(
        jnp.where(
            is_upper[None, :],
            (upper_ids[:, None] >> upper_shift[None, :] & 1) << places[None, :],
            0,
        ),
        axis=1,
    )
    global_shift = jnp.clip(marginal_qubits - local_bits, 0, 30)
    global_code = jnp.sum(jnp.where(is_global, (position >> global_shift & 1) << places, 0))
    upper_code = upper_code + global_code
    bin_ids = jnp.arange(bin_count, dtype=jnp.int32)
    lower_hot = (lower_code[:, None] == bin_ids[None, :]).astype(jnp.float32)
    upper_hot = (upper_code[:, None] == bin_ids[None, :]).astype(jnp.float32)
    folded = jnp.dot(
        weight.reshape(upper_size, lower_size), lower_hot, precision=lax.Precision.HIGHEST
    )
    joint = jnp.dot(upper_hot.T, folded, precision=lax.Precision.HIGHEST)
    lower_mask = jnp.sum(jnp.where(is_lower, 1 << places, 0))
    column_ids = bin_ids & lower_mask
    line_ids = bin_ids - column_ids
    partial_value = jnp.take(
        joint.reshape(bin_count * bin_count), line_ids * bin_count + column_ids
    )
    fidelity_part = jnp.sum(values)
    summed_hist, total = (
        one_axis_at_a_time(partial_value, DEV),
        one_axis_at_a_time(fidelity_part, DEV),
    )
    norm = jnp.sum(summed_hist)
    mine = lax.dynamic_slice_in_dim(summed_hist, position * per_device, per_device)
    amps_total = float(amps_local * devices)
    sample_probs = amps_total * (values / norm)
    histogram = float(bin_count) * (mine / norm)
    fidelity = amps_total * (total / norm) / float(samp_local * devices) - 1.0
    return (sample_probs, histogram, fidelity)


def solution(mesh):
    split = Mesh(mesh.devices.reshape(4, 4, 4, 2), ("dev_0", "dev_1", "dev_2", "dev_3"))
    in_specs = (P(None, DEV), P(), P(DEV, None), P(DEV), P())
    out_specs = (P(DEV), P(DEV), P())
    return jax.shard_map(
        on_device, mesh=split, in_specs=in_specs, out_specs=out_specs, check_vma=False
    )
```

profile of v0, /device:TPU:1, one launch (start us, length us, event | category | flops | bytes accessed | tf_op | source)
XLA Modules:
  0.0 279.6 jit_solution(6741611749301195655)
XLA Ops:
  15.6 11.5 %all-to-all-start.1 = ((f32[2,128,256]{2,0,1:T(2,128)}), f32[2,128,256]{2,0,1:T(2,128)S(1)}, u32[]{:S(2)}, u32[]{:S(2)}) async-start(f32[2,128,256]{2,0,1:T(2,128)} %pad_maximum_fusion), calls=%async_computation.1 | async-start | bytes 524288 | tf_op jit(solution)/shard_map/all_to_all | solution.py:99
  34.6 6.5 %fusion.25 = s32[128,1,256]{2,0,1:T(8,128)S(1)} fusion(f32[8192]{0:T(1024)S(1)} %bitcast.160, f32[8192]{0:T(1024)S(1)} %add_convert_fusion, s32[8192]{0:T(1024)S(1)} %bitcast.158), kind=kOutput, calls=%fused_computation.48 | convolution fusion | flops 3225485312 | bytes 229376 | tf_op jit(solution)/shard_map/dot_general | solution.py:134
  41.1 4.0 %multiply_add_fusion = (f32[64,2,64,2]{3,2,1,0:T(8,128)}, f32[64,2,64,2]{3,2,1,0:T(8,128)}) fusion(f32[2,2]{1,0:T(2,128)S(1)} %get-tuple-element.87, f32[64,64]{1,0:T(8,128)S(1)} %add.414, f32[2,2]{1,0:T(2,128)S(1)} %get-tuple-element.81, f32[64,64]{1,0:T(8,128)S(1)} %sub.311), kind=kLoop, calls=%fused_computation.22 | loop fusion | flops 98304 | bytes 163872 | tf_op jit(solution)/shard_map/add | solution.py:45
  45.8 4.2 %sub.313 = f32[128,128]{1,0:T(8,128)S(1)} reshape(f32[64,2,64,2]{3,2,1,0:T(8,128)} %get-tuple-element.112) | data formatting | bytes 131072 | tf_op jit(solution)/shard_map/sub | solution.py:44
  50.0 4.0 %add.416 = f32[128,128]{1,0:T(8,128)S(1)} reshape(f32[64,2,64,2]{3,2,1,0:T(8,128)} %get-tuple-element.111) | data formatting | bytes 131072 | tf_op jit(solution)/shard_map/add | solution.py:45
  54.8 9.8 %all-to-all-start = ((s32[128,1,256]{2,1,0:T(1,128)}), s32[128,1,256]{2,1,0:T(1,128)S(1)}, u32[]{:S(2)}, u32[]{:S(2)}) async-start(s32[128,1,256]{2,1,0:T(1,128)} %copy.29), calls=%async_computation | async-start | bytes 262144 | tf_op jit(solution)/shard_map/all_to_all | solution.py:138
  67.2 7.6 %all-to-all-done = s32[128,1,256]{2,1,0:T(1,128)S(1)} async-done(((s32[128,1,256]{2,1,0:T(1,128)}), s32[128,1,256]{2,1,0:T(1,128)S(1)}, u32[]{:S(2)}, u32[]{:S(2)}) %all-to-all-start) | async-done | bytes 131104 | tf_op jit(solution)/shard_map/all_to_all | solution.py:138
  74.9 4.1 %all-to-all-start.2 = ((f32[2,128,256]{2,0,1:T(2,128)}), f32[2,128,256]{2,0,1:T(2,128)S(1)}, u32[]{:S(2)}, u32[]{:S(2)}) async-start(f32[2,128,256]{2,0,1:T(2,128)} %copy.38), calls=%async_computation.2 | async-start | bytes 524288 | tf_op jit(solution)/shard_map/all_to_all | solution.py:104
  80.2 9.9 %all-to-all-done.2 = f32[2,128,256]{2,0,1:T(2,128)S(1)} async-done(((f32[2,128,256]{2,0,1:T(2,128)}), f32[2,128,256]{2,0,1:T(2,128)S(1)}, u32[]{:S(2)}, u32[]{:S(2)}) %all-to-all-start.2) | async-done | bytes 262176 | tf_op jit(solution)/shard_map/all_to_all | solution.py:104
  92.9 2.9 %copy.43 = f32[128,8,8,128]{3,1,2,0:T(8,128)} copy(f32[128,8,8,128]{3,2,1,0:T(8,128)S(1)} %convolution_bitcast_fusion) | data formatting | bytes 8388608
  95.9 112.7 %while.11 = (s32[]{:T(128)}, f32[32,1024]{1,0:T(8,128)S(1)}, s32[32,1024]{1,0:T(8,128)S(1)}, f32[256,128]{1,0:T(8,128)S(1)}, s32[]{:T(128)}, /*index=5*/s32[]{:T(128)}) while((s32[]{:T(128)}, f32[32,1024]{1,0:T(8,128)S(1)}, s32[32,1024]{1,0:T(8,128)S(1)}, f32[256,128]{1,0:T(8,128)S(1)}, s32[]{:T(128)}, /*index=5*/s32[]{:T(128)}) %tuple.102), condition=%wide.region_5.6_spmd.clone, body=%wide.region_3.5_spmd.clone.sunk | while | flops 535554 | bytes 1628241 | solution.py:73
  95.9 2.8 %gather_fusion = f32[1024,128]{1,0:T(8,128)S(1)} fusion(f32[256,128]{1,0:T(8,128)S(1)} %get-tuple-element.206, s32[1024]{0:T(1024)S(1)} %broadcast_clamp_fusion.3), kind=kCustom, calls=%fused_computation.clone.clone.1 | custom fusion | bytes 1052672 | tf_op jit(solution)/shard_map/while/body/eval_jaxpr/jit(_take)/gather | solution.py:68
  99.4 2.8 %gather_fusion = f32[1024,128]{1,0:T(8,128)S(1)} fusion(f32[256,128]{1,0:T(8,128)S(1)} %get-tuple-element.206, s32[1024]{0:T(1024)S(1)} %broadcast_clamp_fusion.3), kind=kCustom, calls=%fused_computation.clone.clone.1 | custom fusion | bytes 1052672 | tf_op jit(solution)/shard_map/while/body/eval_jaxpr/jit(_take)/gather | solution.py:68
  102.9 2.8 %gather_fusion = f32[1024,128]{1,0:T(8,128)S(1)} fusion(f32[256,128]{1,0:T(8,128)S(1)} %get-tuple-element.206, s32[1024]{0:T(1024)S(1)} %broadcast_clamp_fusion.3), kind=kCustom, calls=%fused_computation.clone.clone.1 | custom fusion | bytes 1052672 | tf_op jit(solution)/shard_map/while/body/eval_jaxpr/jit(_take)/gather | solution.py:68
  106.5 2.8 %gather_fusion = f32[1024,128]{1,0:T(8,128)S(1)} fusion(f32[256,128]{1,0:T(8,128)S(1)} %get-tuple-element.206, s32[1024]{0:T(1024)S(1)} %broadcast_clamp_fusion.3), kind=kCustom, calls=%fused_computation.clone.clone.1 | custom fusion | bytes 1052672 | tf_op jit(solution)/shard_map/while/body/eval_jaxpr/jit(_take)/gather | solution.py:68
  110.0 2.8 %gather_fusion = f32[1024,128]{1,0:T(8,128)S(1)} fusion(f32[256,128]{1,0:T(8,128)S(1)} %get-tuple-element.206, s32[1024]{0:T(1024)S(1)} %broadcast_clamp_fusion.3), kind=kCustom, calls=%fused_computation.clone.clone.1 | custom fusion | bytes 1052672 | tf_op jit(solution)/shard_map/while/body/eval_jaxpr/jit(_take)/gather | solution.py:68
  113.5 2.8 %gather_fusion = f32[1024,128]{1,0:T(8,128)S(1)} fusion(f32[256,128]{1,0:T(8,128)S(1)} %get-tuple-element.206, s32[1024]{0:T(1024)S(1)} %broadcast_clamp_fusion.3), kind=kCustom, calls=%fused_computation.clone.clone.1 | custom fusion | bytes 1052672 | tf_op jit(solution)/shard_map/while/body/eval_jaxpr/jit(_take)/gather | solution.py:68
  117.0 2.8 %gather_fusion = f32[1024,128]{1,0:T(8,128)S(1)} fusion(f32[256,128]{1,0:T(8,128)S(1)} %get-tuple-element.206, s32[1024]{0:T(1024)S(1)} %broadcast_clamp_fusion.3), kind=kCustom, calls=%fused_computation.clone.clone.1 | custom fusion | bytes 1052672 | tf_op jit(solution)/shard_map/while/body/eval_jaxpr/jit(_take)/gather | solution.py:68
  120.6 2.8 %gather_fusion = f32[1024,128]{1,0:T(8,128)S(1)} fusion(f32[256,128]{1,0:T(8,128)S(1)} %get-tuple-element.206, s32[1024]{0:T(1024)S(1)} %broadcast_clamp_fusion.3), kind=kCustom, calls=%fused_computation.clone.clone.1 | custom fusion | bytes 1052672 | tf_op jit(solution)/shard_map/while/body/eval_jaxpr/jit(_take)/gather | solution.py:68
  124.1 2.8 %gather_fusion = f32[1024,128]{1,0:T(8,128)S(1)} fusion(f32[256,128]{1,0:T(8,128)S(1)} %get-tuple-element.206, s32[1024]{0:T(1024)S(1)} %broadcast_clamp_fusion.3), kind=kCustom, calls=%fused_computation.clone.clone.1 | custom fusion | bytes 1052672 | tf_op jit(solution)/shard_map/while/body/eval_jaxpr/jit(_take)/gather | solution.py:68
  127.6 2.8 %gather_fusion = f32[1024,128]{1,0:T(8,128)S(1)} fusion(f32[256,128]{1,0:T(8,128)S(1)} %get-tuple-element.206, s32[1024]{0:T(1024)S(1)} %broadcast_clamp_fusion.3), kind=kCustom, calls=%fused_computation.clone.clone.1 | custom fusion | bytes 1052672 | tf_op jit(solution)/shard_map/while/body/eval_jaxpr/jit(_take)/gather | solution.py:68
  131.1 2.8 %gather_fusion = f32[1024,128]{1,0:T(8,128)S(1)} fusion(f32[256,128]{1,0:T(8,128)S(1)} %get-tuple-element.206, s32[1024]{0:T(1024)S(1)} %broadcast_clamp_fusion.3), kind=kCustom, calls=%fused_computation.clone.clone.1 | custom fusion | bytes 1052672 | tf_op jit(solution)/shard_map/while/body/eval_jaxpr/jit(_take)/gather | solution.py:68
  134.6 2.8 %gather_fusion = f32[1024,128]{1,0:T(8,128)S(1)} fusion(f32[256,128]{1,0:T(8,128)S(1)} %get-tuple-element.206, s32[1024]{0:T(1024)S(1)} %broadcast_clamp_fusion.3), kind=kCustom, calls=%fused_computation.clone.clone.1 | custom fusion | bytes 1052672 | tf_op jit(solution)/shard_map/while/body/eval_jaxpr/jit(_take)/gather | solution.py:68
  138.2 2.8 %gather_fusion = f32[1024,128]{1,0:T(8,128)S(1)} fusion(f32[256,128]{1,0:T(8,128)S(1)} %get-tuple-element.206, s32[1024]{0:T(1024)S(1)} %broadcast_clamp_fusion.3), kind=kCustom, calls=%fused_computation.clone.clone.1 | custom fusion | bytes 1052672 | tf_op jit(solution)/shard_map/while/body/eval_jaxpr/jit(_take)/gather | solution.py:68
  141.7 2.8 %gather_fusion = f32[1024,128]{1,0:T(8,128)S(1)} fusion(f32[256,128]{1,0:T(8,128)S(1)} %get-tuple-element.206, s32[1024]{0:T(1024)S(1)} %broadcast_clamp_fusion.3), kind=kCustom, calls=%fused_computation.clone.clone.1 | custom fusion | bytes 1052672 | tf_op jit(solution)/shard_map/while/body/eval_jaxpr/jit(_take)/gather | solution.py:68
  145.2 2.8 %gather_fusion = f32[1024,128]{1,0:T(8,128)S(1)} fusion(f32[256,128]{1,0:T(8,128)S(1)} %get-tuple-element.206, s32[1024]{0:T(1024)S(1)} %broadcast_clamp_fusion.3), kind=kCustom, calls=%fused_computation.clone.clone.1 | custom fusion | bytes 1052672 | tf_op jit(solution)/shard_map/while/body/eval_jaxpr/jit(_take)/gather | solution.py:68
  148.7 2.8 %gather_fusion = f32[1024,128]{1,0:T(8,128)S(1)} fusion(f32[256,128]{1,0:T(8,128)S(1)} %get-tuple-element.206, s32[1024]{0:T(1024)S(1)} %broadcast_clamp_fusion.3), kind=kCustom, calls=%fused_computation.clone.clone.1 | custom fusion | bytes 1052672 | tf_op jit(solution)/shard_map/while/body/eval_jaxpr/jit(_take)/gather | solution.py:68
  152.3 2.8 %gather_fusion = f32[1024,128]{1,0:T(8,128)S(1)} fusion(f32[256,128]{1,0:T(8,128)S(1)} %get-tuple-element.206, s32[1024]{0:T(1024)S(1)} %broadcast_clamp_fusion.3), kind=kCustom, calls=%fused_computation.clone.clone.1 | custom fusion | bytes 1052672 | tf_op jit(solution)/shard_map/while/body/eval_jaxpr/jit(_take)/gather | solution.py:68
  155.8 2.8 %gather_fusion = f32[1024,128]{1,0:T(8,128)S(1)} fusion(f32[256,128]{1,0:T(8,128)S(1)} %get-tuple-element.206, s32[1024]{0:T(1024)S(1)} %broadcast_clamp_fusion.3), kind=kCustom, calls=%fused_computation.clone.clone.1 | custom fusion | bytes 1052672 | tf_op jit(solution)/shard_map/while/body/eval_jaxpr/jit(_take)/gather | solution.py:68
  159.3 2.8 %gather_fusion = f32[1024,128]{1,0:T(8,128)S(1)} fusion(f32[256,128]{1,0:T(8,128)S(1)} %get-tuple-element.206, s32[1024]{0:T(1024)S(1)} %broadcast_clamp_fusion.3), kind=kCustom, calls=%fused_computation.clone.clone.1 | custom fusion | bytes 1052672 | tf_op jit(solution)/shard_map/while/body/eval_jaxpr/jit(_take)/gather | solution.py:68
  162.8 2.8 %gather_fusion = f32[1024,128]{1,0:T(8,128)S(1)} fusion(f32[256,128]{1,0:T(8,128)S(1)} %get-tuple-element.206, s32[1024]{0:T(1024)S(1)} %broadcast_clamp_fusion.3), kind=kCustom, calls=%fused_computation.clone.clone.1 | custom fusion | bytes 1052672 | tf_op jit(solution)/shard_map/while/body/eval_jaxpr/jit(_take)/gather | solution.py:68
  166.3 2.8 %gather_fusion = f32[1024,128]{1,0:T(8,128)S(1)} fusion(f32[256,128]{1,0:T(8,128)S(1)} %get-tuple-element.206, s32[1024]{0:T(1024)S(1)} %broadcast_clamp_fusion.3), kind=kCustom, calls=%fused_computation.clone.clone.1 | custom fusion | bytes 1052672 | tf_op jit(solution)/shard_map/while/body/eval_jaxpr/jit(_take)/gather | solution.py:68
  169.9 2.8 %gather_fusion = f32[1024,128]{1,0:T(8,128)S(1)} fusion(f32[256,128]{1,0:T(8,128)S(1)} %get-tuple-element.206, s32[1024]{0:T(1024)S(1)} %broadcast_clamp_fusion.3), kind=kCustom, calls=%fused_computation.clone.clone.1 | custom fusion | bytes 1052672 | tf_op jit(solution)/shard_map/while/body/eval_jaxpr/jit(_take)/gather | solution.py:68
  173.4 2.8 %gather_fusion = f32[1024,128]{1,0:T(8,128)S(1)} fusion(f32[256,128]{1,0:T(8,128)S(1)} %get-tuple-element.206, s32[1024]{0:T(1024)S(1)} %broadcast_clamp_fusion.3), kind=kCustom, calls=%fused_computation.clone.clone.1 | custom fusion | bytes 1052672 | tf_op jit(solution)/shard_map/while/body/eval_jaxpr/jit(_take)/gather | solution.py:68
  176.9 2.8 %gather_fusion = f32[1024,128]{1,0:T(8,128)S(1)} fusion(f32[256,128]{1,0:T(8,128)S(1)} %get-tuple-element.206, s32[1024]{0:T(1024)S(1)} %broadcast_clamp_fusion.3), kind=kCustom, calls=%fused_computation.clone.clone.1 | custom fusion | bytes 1052672 | tf_op jit(solution)/shard_map/while/body/eval_jaxpr/jit(_take)/gather | solution.py:68
  180.4 2.8 %gather_fusion = f32[1024,128]{1,0:T(8,128)S(1)} fusion(f32[256,128]{1,0:T(8,128)S(1)} %get-tuple-element.206, s32[1024]{0:T(1024)S(1)} %broadcast_clamp_fusion.3), kind=kCustom, calls=%fused_computation.clone.clone.1 | custom fusion | bytes 1052672 | tf_op jit(solution)/shard_map/while/body/eval_jaxpr/jit(_take)/gather | solution.py:68
  184.0 2.8 %gather_fusion = f32[1024,128]{1,0:T(8,128)S(1)} fusion(f32[256,128]{1,0:T(8,128)S(1)} %get-tuple-element.206, s32[1024]{0:T(1024)S(1)} %broadcast_clamp_fusion.3), kind=kCustom, calls=%fused_computation.clone.clone.1 | custom fusion | bytes 1052672 | tf_op jit(solution)/shard_map/while/body/eval_jaxpr/jit(_take)/gather | solution.py:68
  187.5 2.8 %gather_fusion = f32[1024,128]{1,0:T(8,128)S(1)} fusion(f32[256,128]{1,0:T(8,128)S(1)} %get-tuple-element.206, s32[1024]{0:T(1024)S(1)} %broadcast_clamp_fusion.3), kind=kCustom, calls=%fused_computation.clone.clone.1 | custom fusion | bytes 1052672 | tf_op jit(solution)/shard_map/while/body/eval_jaxpr/jit(_take)/gather | solution.py:68
  191.0 2.8 %gather_fusion = f32[1024,128]{1,0:T(8,128)S(1)} fusion(f32[256,128]{1,0:T(8,128)S(1)} %get-tuple-element.206, s32[1024]{0:T(1024)S(1)} %broadcast_clamp_fusion.3), kind=kCustom, calls=%fused_computation.clone.clone.1 | custom fusion | bytes 1052672 | tf_op jit(solution)/shard_map/while/body/eval_jaxpr/jit(_take)/gather | solution.py:68
  198.0 2.8 %gather_fusion = f32[1024,128]{1,0:T(8,128)S(1)} fusion(f32[256,128]{1,0:T(8,128)S(1)} %get-tuple-element.206, s32[1024]{0:T(1024)S(1)} %broadcast_clamp_fusion.3), kind=kCustom, calls=%fused_computation.clone.clone.1 | custom fusion | bytes 1052672 | tf_op jit(solution)/shard_map/while/body/eval_jaxpr/jit(_take)/gather | solution.py:68
  201.6 2.8 %gather_fusion = f32[1024,128]{1,0:T(8,128)S(1)} fusion(f32[256,128]{1,0:T(8,128)S(1)} %get-tuple-element.206, s32[1024]{0:T(1024)S(1)} %broadcast_clamp_fusion.3), kind=kCustom, calls=%fused_computation.clone.clone.1 | custom fusion | bytes 1052672 | tf_op jit(solution)/shard_map/while/body/eval_jaxpr/jit(_take)/gather | solution.py:68
  209.6 4.3 %all-to-all-start.3 = ((f32[128,1,256]{2,1,0:T(1,128)}), f32[128,1,256]{2,1,0:T(1,128)S(1)}, u32[]{:S(2)}, u32[]{:S(2)}) async-start(f32[128,1,256]{2,1,0:T(1,128)} %compare_select_fusion.2), calls=%async_computation.3 | async-start | bytes 262144 | tf_op jit(solution)/shard_map/all_to_all | solution.py:141
  213.9 15.4 %gather_fusion.1 = f32[1024]{0:T(1024)S(1)} fusion(f32[1048576]{0:T(1024)} %bitcast.153, s32[1024]{0:T(1024)S(1)} %broadcast_clamp_fusion.1), kind=kCustom, calls=%fused_computation.1 | custom fusion | bytes 12288 | tf_op jit(solution)/shard_map/jit(_take)/gather | solution.py:188
  229.9 6.4 %fusion.144 = (f32[]{:T(128)}, f32[8192]{0:T(1024)S(1)}) fusion(f32[128,1,256]{2,1,0:T(1,128)S(1)} %all-to-all-done.3, s32[8192]{0:T(1024)S(1)} %bitcast.159, f32[8192]{0:T(1024)S(1)} %bitcast.161), kind=kOutput, calls=%fused_computation.323 | convolution fusion | flops 3230654464 | bytes 229380 | tf_op jit(solution)/shard_map/dot_general | solution.py:143
  236.3 9.9 %all-reduce.3 = (f32[1024]{0:T(1024)S(1)}, f32[]{:T(128)}) all-reduce(f32[1024]{0:T(1024)S(1)} %fusion.55, f32[]{:T(128)} %get-tuple-element.41), channel_id=1, replica_groups=mesh['dev_0'=4,'dev_1'=4,'dev_2'=4,'dev_3'=2] {'dev_0'}, use_global_device_ids=true, to_apply=%region_11.12 | all-reduce | flops 1025 | bytes 8200 | tf_op jit(solution)/shard_map/psum | solution.py:12
  246.2 9.2 %all-reduce.2 = (f32[1024]{0:T(1024)S(1)}, f32[]{:T(128)}) all-reduce(f32[1024]{0:T(1024)S(1)} %get-tuple-element.103, f32[]{:T(128)} %get-tuple-element.104), channel_id=1, replica_groups=mesh['dev_0'=4,'dev_1'=4,'dev_2'=4,'dev_3'=2] {'dev_1'}, use_global_device_ids=true, to_apply=%region_12.13 | all-reduce | flops 1025 | bytes 8200 | tf_op jit(solution)/shard_map/psum | solution.py:12
  255.4 9.3 %all-reduce.1 = (f32[1024]{0:T(1024)S(1)}, f32[]{:T(128)}) all-reduce(f32[1024]{0:T(1024)S(1)} %get-tuple-element.101, f32[]{:T(128)} %get-tuple-element.102), channel_id=1, replica_groups=mesh['dev_0'=4,'dev_1'=4,'dev_2'=4,'dev_3'=2] {'dev_2'}, use_global_device_ids=true, to_apply=%region_13.14 | all-reduce | flops 1025 | bytes 8200 | tf_op jit(solution)/shard_map/psum | solution.py:12
  264.7 9.2 %all-reduce.4 = (f32[1024]{0:T(1024)S(1)}, f32[]{:T(128)}) all-reduce(f32[1024]{0:T(1024)S(1)} %get-tuple-element.99, f32[]{:T(128)} %get-tuple-element.100), channel_id=1, replica_groups=mesh['dev_0'=4,'dev_1'=4,'dev_2'=4,'dev_3'=2] {'dev_3'}, use_global_device_ids=true, to_apply=%region_14.15 | all-reduce | flops 1025 | bytes 8200 | tf_op jit(solution)/shard_map/psum | solution.py:12
  (324 shorter events, 61.5 us)
Async XLA Ops:
  0.6 3.9 %copy-start = (f32[2,32768]{1,0:T(2,128)S(1)}, f32[2,32768]{1,0:T(2,128)}, u32[]{:S(2)}) copy-start(f32[2,32768]{1,0:T(2,128)} %param.7) | copy-start | bytes 786436
  13.5 16.8 %copy-start.3 = (s32[10]{0:T(128)S(1)}, s32[10]{0:T(128)}, u32[]{:S(2)}) copy-start(s32[10]{0:T(128)} %param.11) | copy-start | bytes 124
  13.5 18.0 %copy-start.2 = (s32[8192,1]{0,1:T(1,128)S(1)}, s32[8192,1]{0,1:T(1,128)}, u32[]{:S(2)}) copy-start(s32[8192,1]{0,1:T(1,128)} %param.9) | copy-start | bytes 98308
  15.6 39.2 %all-to-all-start.1 = ((f32[2,128,256]{2,0,1:T(2,128)}), f32[2,128,256]{2,0,1:T(2,128)S(1)}, u32[]{:S(2)}, u32[]{:S(2)}) async-start(f32[2,128,256]{2,0,1:T(2,128)} %pad_maximum_fusion), calls=%async_computation.1 | async-start | bytes 524288 | tf_op jit(solution)/shard_map/all_to_all | solution.py:99
  32.8 1.7 copy-start.1
  54.8 20.0 %all-to-all-start = ((s32[128,1,256]{2,1,0:T(1,128)}), s32[128,1,256]{2,1,0:T(1,128)S(1)}, u32[]{:S(2)}, u32[]{:S(2)}) async-start(s32[128,1,256]{2,1,0:T(1,128)} %copy.29), calls=%async_computation | async-start | bytes 262144 | tf_op jit(solution)/shard_map/all_to_all | solution.py:138
  74.9 15.2 %all-to-all-start.2 = ((f32[2,128,256]{2,0,1:T(2,128)}), f32[2,128,256]{2,0,1:T(2,128)S(1)}, u32[]{:S(2)}, u32[]{:S(2)}) async-start(f32[2,128,256]{2,0,1:T(2,128)} %copy.38), calls=%async_computation.2 | async-start | bytes 524288 | tf_op jit(solution)/shard_map/all_to_all | solution.py:104
  209.6 20.3 %all-to-all-start.3 = ((f32[128,1,256]{2,1,0:T(1,128)}), f32[128,1,256]{2,1,0:T(1,128)S(1)}, u32[]{:S(2)}, u32[]{:S(2)}) async-start(f32[128,1,256]{2,1,0:T(1,128)} %compare_select_fusion.2), calls=%async_computation.3 | async-start | bytes 262144 | tf_op jit(solution)/shard_map/all_to_all | solution.py:141
where the time goes:
time: 281 us; the launch traced here: 280 us
  local copies, waits for them, and re-layouts  131 us (47%)
  blocking collectives  37.6 us (13%)
  other arithmetic  35.3 us (13%)
  starting transfers between devices  29.7 us (11%)
  matrix products  22.8 us (8%)
  waiting for transfers between devices  17.5 us (6%)
  between operations  3.73 us (1%)
    gather x32, local copies, waits for them, and re-layouts, one_block(): picked = jnp.take(weight_rows, upper, axis=0)  89.8 us
    psum x4, blocking collectives, one_axis_at_a_time(): shard = lax.psum(shard, axis)  37.6 us
    reduce_sum x32, other arithmetic, one_block(): jnp.sum(jnp.where(lower[:, None] == lane_ids[None, :], picked, 0.0), axis=1)  15.9 us
    gather x1, local copies, waits for them, and re-layouts, on_device(): jnp.take(joint.reshape(bin_count * bin_count), line_ids * bin_count + col...  15.4 us
    all_to_all x1, starting transfers between devices, on_device(): lax.all_to_all(stacked, DEV, split_axis=1, concat_axis=1, tiled=True)  11.5 us
    all_to_all x1, waiting for transfers between devices, on_device(): lax.all_to_all(jnp.stack([new_real[0], new_imag[0]]), DEV, split_axis=1,...  9.92 us
    all_to_all x1, starting transfers between devices, on_device(): lax.all_to_all(requests, DEV, split_axis=0, concat_axis=0, tiled=True)  9.76 us
    all_to_all x1, waiting for transfers between devices, on_device(): lax.all_to_all(requests, DEV, split_axis=0, concat_axis=0, tiled=True)  7.63 us
  transfers between devices with their start and end apart: 4, of which 2 were waited for; matrix products, arithmetic and copies ran while one was open for 17% of the time, Pallas kernels for 0%

commit v1 on v0

v1 whole, which is shorter than its diff:
```python
import functools

import jax
import jax.numpy as jnp
from jax import lax
from jax.experimental import pallas as pl
from jax.experimental.pallas import tpu as pltpu
from jax.sharding import PartitionSpec as P

N = 128
MESH = pl.DeviceIdType.MESH
F32 = jnp.float32
BF16 = jnp.bfloat16
I32 = jnp.int32


def iota(shape, dim):
    return lax.broadcasted_iota(I32, shape, dim)


def dot(a, b):
    return jnp.dot(a, b, preferred_element_type=F32)


def split(x):
    high = x.astype(BF16)
    low = (x - high.astype(F32)).astype(BF16)
    return high, low


def dot3(a, b):
    a_high, a_low = split(a)
    b_high, b_low = split(b)
    return dot(a_high, b_high) + (dot(a_high, b_low) + dot(a_low, b_high))


def complex_mul(a, b):
    return (a[0] * b[0] - a[1] * b[1], a[0] * b[1] + a[1] * b[0])


def gate_entries(angles):
    rows = angles.shape[0]
    lane = iota((rows, 128), 1)
    theta, first, second = (
        jnp.broadcast_to(angles[:, k : k + 1], (rows, 128)) for k in range(3)
    )
    packed = jnp.where(
        lane == 0, theta, jnp.where(lane == 1, first, jnp.where(lane == 2, second, first + second))
    )
    sines, cosines = jnp.sin(packed), jnp.cos(packed)

    def column(x, k):
        return jnp.broadcast_to(x[:, k : k + 1], (rows, 128))

    ct, st = column(cosines, 0), column(sines, 0)
    return [
        (ct, jnp.zeros_like(ct)),
        (-column(cosines, 2) * st, -column(sines, 2) * st),
        (column(cosines, 1) * st, column(sines, 1) * st),
        (column(cosines, 3) * ct, column(sines, 3) * ct),
    ]


def kron_matrix(entry, qubits, transposed):
    size = 2 ** len(qubits)
    lane, sub = iota((8, size), 1), iota((8, size), 0)

    def factor_rows(place, qubit):
        bit = (lane >> place) & 1 == 1

        def choose(zero, one):
            return tuple(
                jnp.where(bit, entry(one, part, qubit, size), entry(zero, part, qubit, size))
                for part in range(2)
            )

        if transposed:
            return choose(0, 2), choose(1, 3)
        return choose(0, 1), choose(2, 3)

    mat = None
    for place, qubit in enumerate(qubits):
        row_zero, row_one = factor_rows(place, qubit)
        if place < 3:
            bit = (sub >> place) & 1 == 1
            factor = tuple(jnp.where(bit, row_one[k], row_zero[k]) for k in range(2))
            mat = factor if mat is None else complex_mul(mat, factor)
        else:
            count = mat[0].shape[0] // 8
            halves = []
            for row in (row_zero, row_one):
                wide = tuple(jnp.concatenate([x] * count, axis=0) for x in row)
                halves.append(complex_mul(mat, wide))
            mat = tuple(jnp.concatenate([halves[0][k], halves[1][k]], axis=0) for k in range(2))
    return mat


def select_rows(values, bits):
    for bit in bits:
        half = values.shape[0] // 2
        values = jnp.where(bit, values[half:], values[:half])
    return values


def pick_sublane(values, index):
    hit = iota(values.shape, 0) == index
    return jnp.sum(jnp.where(hit, values, 0.0), axis=0, keepdims=True)


def bit_of(x, place):
    return (x >> place) & 1 == 1


def kernel(
    state_ref, angles_ref, high_ref, low_ref, marg_ref,
    probs_ref, hist_ref, fid_ref,
    gate_ref, send_amp, recv_amp, send_req, recv_req, send_wgt, recv_wgt,
    send_hst, recv_hst, send_ans, recv_ans, rank_hot, carry_ref, place_ref,
    send_sem, recv_sem,
):
    me = lax.axis_index("dev")
    barrier = pltpu.get_barrier_semaphore()

    def greet(k, c):
        pl.semaphore_signal(
            barrier, inc=1, device_id=(lax.rem(me + k, N),), device_id_type=MESH
        )
        return c

    lax.fori_loop(1, N, greet, 0)

    def exchange(which, src, dst, rows, pitch, src_block=None):
        def source(d):
            start = d * pitch if src_block is None else src_block(d)
            return src.at[pl.ds(start, rows), :]

        def send(k, c):
            d = lax.rem(me + k, N)
            pltpu.make_async_remote_copy(
                src_ref=source(d),
                dst_ref=dst.at[pl.ds(me * pitch, rows), :],
                send_sem=send_sem.at[which],
                recv_sem=recv_sem.at[which],
                device_id=(d,),
                device_id_type=MESH,
            ).start()
            return c

        lax.fori_loop(1, N, send, 0)
        pltpu.make_async_copy(
            source(me), dst.at[pl.ds(me * pitch, rows), :], recv_sem.at[which]
        ).start()

    def arrived(which, dst, rows):
        whole = dst.at[pl.ds(0, N * rows), :]
        pltpu.make_async_copy(whole, whole, recv_sem.at[which]).wait()

    def sent(which, dst, rows):
        most = dst.at[pl.ds(0, (N - 1) * rows), :]
        pltpu.make_async_copy(most, most, send_sem.at[which]).wait()

    entries = gate_entries(angles_ref[...])
    for kind in range(4):
        for part in range(2):
            gate_ref[2 * kind + part, pl.ds(0, 22), :] = entries[kind][part]

    def entry(kind, part, qubit, size):
        row = gate_ref[2 * kind + part, pl.ds(qubit, 1), :]
        row = jnp.broadcast_to(row, (8, 128))
        return row if size == 128 else jnp.concatenate([row] * (size // 128), axis=1)

    lane_re, lane_im = kron_matrix(entry, list(range(0, 7)), True)
    row_re, row_im = kron_matrix(entry, list(range(7, 15)), False)
    field = jnp.concatenate(
        [state_ref[pl.ds(0, 256, stride=2), :], state_ref[pl.ds(1, 256, stride=2), :]], axis=1
    )
    lane_gate = jnp.concatenate(
        [
            jnp.concatenate([lane_re, lane_im], axis=1),
            jnp.concatenate([-lane_im, lane_re], axis=1),
        ],
        axis=0,
    )
    field = dot3(field, lane_gate)
    product = dot3(jnp.concatenate([row_re, row_im], axis=0), field)
    amp_re = product[:256, :128] - product[256:, 128:]
    amp_im = product[:256, 128:] + product[256:, :128]
    for half in range(2):
        send_amp[pl.ds(half, 128, stride=4), :] = amp_re[half * 128 : (half + 1) * 128]
        send_amp[pl.ds(2 + half, 128, stride=4), :] = amp_im[half * 128 : (half + 1) * 128]
    pl.semaphore_wait(barrier, N - 1)
    exchange(0, send_amp, recv_amp, 4, 4)

    carry_ref[...] = jnp.zeros((128, 256), F32)
    place_ref[...] = jnp.zeros((256, 256), F32)
    before = jnp.where(iota((256, 256), 0) < iota((256, 256), 1), 1.0, 0.0).astype(BF16)
    prefix = jnp.concatenate([before, jnp.ones((256, 256), BF16)], axis=1)

    def route(step, c):
        lhs_parts, hot_parts = [], []
        carry = carry_ref[...]
        for sub in range(4):
            at = step * 8 + 2 * sub
            owner = jnp.concatenate(
                [high_ref[pl.ds(at, 1), :], high_ref[pl.ds(at + 1, 1), :]], axis=1
            )
            low = jnp.concatenate(
                [low_ref[pl.ds(at, 1), :], low_ref[pl.ds(at + 1, 1), :]], axis=1
            )
            mine = iota((128, 256), 0) == owner
            hot = jnp.where(mine, 1.0, 0.0).astype(BF16)
            counts = dot(hot, prefix)
            rank = jnp.sum(
                jnp.where(mine, counts[:, :256] + carry, 0.0), axis=0, keepdims=True
            ).astype(I32)
            carry = carry + counts[:, 256:]
            ranked = jnp.where(iota((256, 256), 0) == rank, 1.0, 0.0).astype(BF16)
            rank_hot[:, pl.ds(pl.multiple_of(step * 1024 + sub * 256, 256), 256)] = ranked
            hot_parts.append(ranked)
            low_part = (low & 255).astype(F32)
            high_part = ((low >> 8) + 1).astype(F32)
            lhs_parts.append(
                jnp.concatenate(
                    [jnp.where(mine, low_part, 0.0), jnp.where(mine, high_part, 0.0)], axis=0
                ).astype(BF16)
            )
        carry_ref[...] = carry
        place_ref[...] += lax.dot_general(
            jnp.concatenate(lhs_parts, axis=1),
            jnp.concatenate(hot_parts, axis=1),
            (((1,), (1,)), ((), ())),
            preferred_element_type=F32,
        )
        return c

    lax.fori_loop(0, 8, route, 0)
    asked = (place_ref[:128, :] + 256.0 * (place_ref[128:, :] - 1.0)).astype(I32)
    for half in range(2):
        send_req[pl.ds(half, 128, stride=2), :] = asked[:, half * 128 : (half + 1) * 128]
    exchange(1, send_req, recv_req, 2, 2)

    glob_re, glob_im = kron_matrix(entry, list(range(15, 22)), False)
    glob = jnp.concatenate(
        [
            jnp.concatenate([glob_re, -glob_im], axis=1),
            jnp.concatenate([glob_im, glob_re], axis=1),
        ],
        axis=0,
    )
    bins = iota((1, 1024), 1)
    local_code = jnp.zeros((256, 128), I32)
    global_code = jnp.zeros((128, 128), I32)
    row_id, g_id = iota((256, 128), 0), iota((128, 128), 0)
    local_mask = jnp.int32(0)
    other_mask = jnp.int32(0)
    other_code = jnp.int32(0)
    for k in range(10):
        qubit = marg_ref[k]
        in_lane, in_dev = qubit < 7, (qubit >= 7) & (qubit < 14)
        in_half, in_glob = qubit == 14, qubit >= 15
        place = jnp.where(in_half, 7, jnp.where(in_lane, qubit, 31))
        local_code += ((row_id >> place) & 1) << k
        local_mask += jnp.where(in_lane | in_half, 1 << k, 0)
        g_place = jnp.where(in_glob, qubit - 15, 31)
        global_code += ((g_id >> g_place) & 1) << k
        other_mask += jnp.where(in_glob | in_dev, 1 << k, 0)
        d_place = jnp.where(in_dev, qubit - 7, 31)
        other_code += ((me >> d_place) & 1) << k
    local_code = jnp.concatenate([local_code] * 8, axis=1)
    global_code = jnp.concatenate([global_code + other_code] * 8, axis=1)
    local_hot = jnp.where((bins & local_mask) == local_code, 1.0, 0.0).astype(BF16)
    global_hit = (bins & other_mask) == global_code

    arrived(0, recv_amp, 4)
    parts = [recv_amp[pl.ds(k, 128, stride=4), :] for k in range(4)]
    spread = jnp.concatenate(
        [
            jnp.concatenate([parts[0], parts[1]], axis=1),
            jnp.concatenate([parts[2], parts[3]], axis=1),
        ],
        axis=0,
    )
    final = dot3(glob, spread)
    weight = final[:128] * final[:128] + final[128:] * final[128:]
    for half in range(2):
        send_wgt[pl.ds(half, 128, stride=2), :] = weight[:, half * 128 : (half + 1) * 128]
    exchange(2, send_wgt, recv_wgt, 2, 2)

    folded = dot(jnp.concatenate(split(weight), axis=0), local_hot)
    folded = jnp.where(global_hit, folded[:128] + folded[128:], 0.0)
    partial = jnp.sum(folded, axis=0, keepdims=True)
    norm_part = jnp.sum(weight[:, :128] + weight[:, 128:], axis=0, keepdims=True)
    for row in range(8):
        send_hst[pl.ds(2 * row, 1), :] = partial[:, row * 128 : (row + 1) * 128]
        send_hst[pl.ds(2 * row + 1, 1), :] = norm_part
    exchange(3, send_hst, recv_hst, 2, 2, lambda d: (d // 16) * 2)

    arrived(1, recv_req, 2)
    arrived(2, recv_wgt, 2)
    table = jnp.concatenate(
        [recv_wgt[pl.ds(half, 128, stride=2), :].T for half in range(2)], axis=0
    )
    table = jnp.concatenate(split(table), axis=1)

    def answer(step, c):
        wanted = []
        for sub in range(16):
            wanted.append(recv_req[pl.ds(step * 16 + sub, 1), :])
        wanted = jnp.concatenate(wanted, axis=1)
        hot = jnp.where(iota((128, 2048), 0) == (wanted >> 7) & 127, 1.0, 0.0).astype(BF16)
        found = dot(table, jnp.concatenate([hot, hot], axis=0))
        found = select_rows(found, [bit_of(wanted, p) for p in (14, 6, 5, 4, 3)])
        found = pick_sublane(found, wanted & 7)
        for sub in range(16):
            at = (step * 8 + sub // 2) * 4 + sub % 2
            send_ans[pl.ds(at, 1), :] = found[:, sub * 128 : (sub + 1) * 128]
        return c

    lax.fori_loop(0, 16, answer, 0)
    fid_part = jnp.zeros((128, 128), F32)
    for half in range(2):
        valid = recv_req[pl.ds(half, 128, stride=2), :] >= 0
        fid_part += jnp.where(valid, send_ans[pl.ds(half, 128, stride=4), :], 0.0)
    fid_part = jnp.sum(fid_part, axis=0, keepdims=True)
    send_ans[pl.ds(2, 128, stride=4), :] = jnp.broadcast_to(fid_part, (128, 128))
    exchange(4, send_ans, recv_ans, 3, 4)

    arrived(3, recv_hst, 2)
    norm = jnp.sum(
        jnp.sum(recv_hst[pl.ds(1, 128, stride=2), :], axis=0, keepdims=True), axis=1, keepdims=True
    )
    bins_row = jnp.sum(recv_hst[pl.ds(0, 128, stride=2), :], axis=0, keepdims=True)
    bins_row = 1024.0 * (bins_row / norm)
    bins_row = pltpu.roll(bins_row, lax.rem(128 - lax.rem(me, 16) * 8, 128), 1)
    hist_ref[...] = bins_row[:, :8]

    arrived(4, recv_ans, 3)
    answers = jnp.concatenate(
        [recv_ans[pl.ds(half, 128, stride=4), :] for half in range(2)], axis=1
    )
    answers = jnp.concatenate(split(answers), axis=0)
    total = jnp.sum(
        jnp.sum(recv_ans[pl.ds(2, 128, stride=4), :], axis=0, keepdims=True), axis=1, keepdims=True
    )
    fid_ref[...] = 4194304.0 * (total / norm) / 1048576.0 - 1.0
    scale = 4194304.0 / norm

    def collect(step, c):
        owner = jnp.concatenate([high_ref[pl.ds(step * 8 + k, 1), :] for k in range(8)], axis=1)
        hot = rank_hot[:, pl.ds(pl.multiple_of(step * 1024, 1024), 1024)]
        found = dot(answers, hot)
        found = found[:128] + found[128:]
        found = select_rows(found, [bit_of(owner, p) for p in (6, 5, 4, 3)])
        found = pick_sublane(found, owner & 7) * scale
        for k in range(8):
            probs_ref[pl.ds(step * 8 + k, 1), :] = found[:, k * 128 : (k + 1) * 128]
        return c

    lax.fori_loop(0, 8, collect, 0)
    sent(0, send_amp, 4)
    sent(1, send_req, 2)
    sent(2, send_wgt, 2)
    sent(3, recv_hst, 2)
    sent(4, send_ans, 3)


def on_device(state, angles, sample_high, sample_low, marginal_qubits):
    vmem = pl.BlockSpec(memory_space=pltpu.VMEM)
    field = state.reshape(2, 256, 128).transpose(1, 0, 2).reshape(512, 128)
    probs, hist, fid = pl.pallas_call(
        kernel,
        out_shape=(
            jax.ShapeDtypeStruct((64, 128), F32),
            jax.ShapeDtypeStruct((1, 8), F32),
            jax.ShapeDtypeStruct((1, 1), F32),
        ),
        in_specs=[vmem, vmem, vmem, vmem, pl.BlockSpec(memory_space=pltpu.SMEM)],
        out_specs=(vmem, vmem, vmem),
        scratch_shapes=[
            pltpu.VMEM((8, 24, 128), F32),
            pltpu.VMEM((512, 128), F32),
            pltpu.VMEM((512, 128), F32),
            pltpu.VMEM((256, 128), I32),
            pltpu.VMEM((256, 128), I32),
            pltpu.VMEM((256, 128), F32),
            pltpu.VMEM((256, 128), F32),
            pltpu.VMEM((16, 128), F32),
            pltpu.VMEM((256, 128), F32),
            pltpu.VMEM((512, 128), F32),
            pltpu.VMEM((512, 128), F32),
            pltpu.VMEM((256, 8192), BF16),
            pltpu.VMEM((128, 256), F32),
            pltpu.VMEM((256, 256), F32),
            pltpu.SemaphoreType.DMA((5,)),
            pltpu.SemaphoreType.DMA((5,)),
        ],
        compiler_params=pltpu.CompilerParams(collective_id=0, has_side_effects=True),
    )(
        field,
        angles,
        sample_high.reshape(64, 128),
        sample_low.reshape(64, 128),
        marginal_qubits,
    )
    return probs.reshape(8192), hist.reshape(8), fid.reshape(())


def solution(mesh):
    return jax.shard_map(
        on_device,
        mesh=mesh,
        in_specs=(P(None, "dev"), P(), P("dev", None), P("dev"), P()),
        out_specs=(P("dev"), P("dev"), P()),
        check_vma=False,
    )
```

time: 281 us -> 52.4 us (0.19)
  local copies, waits for them, and re-layouts: 131 us -> 3.25 us
  Pallas kernels: 0 us -> 46.6 us
  blocking collectives: 37.6 us -> 0 us
  other arithmetic: 35.3 us -> 0 us
  starting transfers between devices: 29.7 us -> 0 us
  matrix products: 22.8 us -> 0 us
  waiting for transfers between devices: 17.5 us -> 0 us
    gather x33 -> x0, local copies, waits for them, and re-layouts: 105 us -> none  [the longest x32 89.8 us: one_block(): picked = jnp.take(weight_rows, upper, axis=0)]
    pallas_call x0 -> x1, Pallas kernels: none -> 46.6 us  [on_device(): pl.pallas_call(kernel, out_shape=(jax.ShapeDtypeStruct((64, 128), F32), j...]
    psum x4 -> x0, blocking collectives: 37.6 us -> none  [one_axis_at_a_time(): shard = lax.psum(shard, axis)]
    all_to_all x4 -> x0, starting transfers between devices: 29.7 us -> none  [the longest x1 11.5 us: on_device(): lax.all_to_all(stacked, DEV, split_axis=1, concat_axis=1, tiled=True)]
    dot_general x21 -> x0, matrix products: 22.8 us -> none  [the longest x1 6.52 us: on_device(): jnp.dot((owner_hot * shifted_low[:, None]).T, rank_hot, precision=lax.Pre...]
    reduce_sum x37 -> x0, other arithmetic: 17.9 us -> none  [the longest x32 15.9 us: one_block(): jnp.sum(jnp.where(lower[:, None] == lane_ids[None, :], picked, 0.0), axis=1)]
    all_to_all x4 -> x0, waiting for transfers between devices: 17.5 us -> none  [the longest x1 9.92 us: on_device(): lax.all_to_all(jnp.stack([new_real[0], new_imag[0]]), DEV, split_axis=1,...]
    sub x19 -> x0, local copies, waits for them, and re-layouts: 7.62 us -> none  [the longest x18 7.49 us: kron_gates(): jnp.kron(mat_real, gate_real[qubit]) - jnp.kron(mat_imag, gate_imag[qubit])]
  transfers between devices with their start and end apart: 4 -> 0, of which waited for: 2 -> 0; matrix products, arithmetic and copies ran while one was open for 17% -> 0% of each run, Pallas kernels for 0% -> 0%
where the time goes in v1:
time: 52.4 us; the launch traced here: 52.1 us
  Pallas kernels  46.6 us (89%)
  local copies, waits for them, and re-layouts  3.25 us (6%)
  between operations  2.34 us (4%)
    pallas_call x1, Pallas kernels, on_device(): pl.pallas_call(kernel, out_shape=(jax.ShapeDtypeStruct((64, 128), F32), j...  46.6 us
    unnamed x7, local copies, waits for them, and re-layouts  3.25 us

profile of v1, /device:TPU:1, one launch (start us, length us, event | category | flops | bytes accessed | tf_op | source)
XLA Modules:
  0.0 52.1 jit_solution(16428560772281200971)
XLA Ops:
  0.6 0.0 copy-start
  0.6 0.7 %copy-done = f32[22,3]{0,1:T(4,128)S(1)} copy-done((f32[22,3]{0,1:T(4,128)S(1)}, f32[22,3]{0,1:T(4,128)}, u32[]{:S(2)}) %copy-start) | copy-done | bytes 288
  1.3 0.7 %copy.9.angles_ref = f32[22,3]{1,0:T(8,128)} copy(f32[22,3]{0,1:T(4,128)S(1)} %copy-done) | data formatting | bytes 528 | tf_op args[1]
  2.0 46.6 %shard_map.76 = (f32[64,128]{1,0:T(8,128)}, f32[1,8]{1,0:T(1,128)}, f32[1,1]{1,0:T(1,128)}) custom-call(f32[512,128]{1,0:T(8,128)} %bitcast.10, f32[22,3]{1,0:T(8,128)} %copy.9.angles_ref, s32[64,128]{1,0:T(8,128)} %bitcast.12, s32[64,128]{1,0:T(8,128)} %bitcast.13, s32[10]{0:T(128)} %marg_ref.1), custom_call_target="tpu_custom_call" | custom-call | tf_op jit(solution)/shard_map/pallas_call | solution.py:370
  48.6 0.0 copy-start.1
  48.6 1.4 %copy.13 = f32[8192]{0:T(1024)} copy(f32[8192]{0:T(1024)} %bitcast.11) | data formatting | bytes 65536
  49.9 0.0 copy-done.1
  49.9 0.5 copy.14
Async XLA Ops:
  0.6 0.7 %copy-start = (f32[22,3]{0,1:T(4,128)S(1)}, f32[22,3]{0,1:T(4,128)}, u32[]{:S(2)}) copy-start(f32[22,3]{0,1:T(4,128)} %param.6) | copy-start | bytes 796
  48.6 1.4 %copy-start.1 = (f32[1,8]{1,0:T(1,128)S(1)}, f32[1,8]{1,0:T(1,128)}, u32[]{:S(2)}) copy-start(f32[1,8]{1,0:T(1,128)} %get-tuple-element.7) | copy-start | bytes 100

commit v2 on v1

--- a/solution.py
+++ b/solution.py
@@ -38,26 +38,23 @@
     return (a[0] * b[0] - a[1] * b[1], a[0] * b[1] + a[1] * b[0])
 
 
-def gate_entries(angles):
-    rows = angles.shape[0]
-    lane = iota((rows, 128), 1)
-    theta, first, second = (
-        jnp.broadcast_to(angles[:, k : k + 1], (rows, 128)) for k in range(3)
-    )
-    packed = jnp.where(
-        lane == 0, theta, jnp.where(lane == 1, first, jnp.where(lane == 2, second, first + second))
-    )
-    sines, cosines = jnp.sin(packed), jnp.cos(packed)
-
-    def column(x, k):
-        return jnp.broadcast_to(x[:, k : k + 1], (rows, 128))
-
-    ct, st = column(cosines, 0), column(sines, 0)
+def gate_entries(angles, trig_ref):
+    count = angles.shape[1]
+    packed = jnp.concatenate([angles, angles[1:2] + angles[2:3]], axis=0)
+    trig_ref[...] = jnp.zeros((8, 128), F32)
+    trig_ref[pl.ds(0, 4), pl.ds(0, count)] = jnp.sin(packed)
+    trig_ref[pl.ds(4, 4), pl.ds(0, count)] = jnp.cos(packed)
+    turned = trig_ref[...].T
+
+    def column(k):
+        return jnp.broadcast_to(turned[:24, k : k + 1], (24, 128))
+
+    sin_t, sin_f, sin_l, sin_fl, cos_t, cos_f, cos_l, cos_fl = (column(k) for k in range(8))
     return [
-        (ct, jnp.zeros_like(ct)),
-        (-column(cosines, 2) * st, -column(sines, 2) * st),
-        (column(cosines, 1) * st, column(sines, 1) * st),
-        (column(cosines, 3) * ct, column(sines, 3) * ct),
+        (cos_t, jnp.zeros_like(cos_t)),
+        (-cos_l * sin_t, -sin_l * sin_t),
+        (cos_f * sin_t, sin_f * sin_t),
+        (cos_fl * cos_t, sin_fl * cos_t),
     ]
 
 
@@ -112,13 +109,28 @@
 
 
 def kernel(
-    state_ref, angles_ref, high_ref, low_ref, marg_ref,
+    state_hbm, angles_hbm, high_hbm, low_hbm, marg_hbm,
     probs_ref, hist_ref, fid_ref,
-    gate_ref, send_amp, recv_amp, send_req, recv_req, send_wgt, recv_wgt,
-    send_hst, recv_hst, send_ans, recv_ans, rank_hot, carry_ref, place_ref,
-    send_sem, recv_sem,
+    state_ref, angles_ref, high_ref, low_ref, marg_ref, trig_ref, gate_ref, send_amp, recv_amp, send_req, recv_req, send_wgt, recv_wgt,
+    send_hst, recv_hst, send_ans, recv_ans, send_fid, recv_fid,
+    rank_hot, rank_ref, seen_ref, place_ref, want_hot,
+    send_sem, recv_sem, load_sem,
 ):
     me = lax.axis_index("dev")
+    loads = [
+        pltpu.make_async_copy(src, dst, load_sem.at[k])
+        for k, (src, dst) in enumerate(
+            [
+                (angles_hbm, angles_ref),
+                (state_hbm, state_ref),
+                (high_hbm, high_ref),
+                (low_hbm, low_ref),
+                (marg_hbm, marg_ref),
+            ]
+        )
+    ]
+    for load in loads:
+        load.start()
     barrier = pltpu.get_barrier_semaphore()
 
     def greet(k, c):
@@ -127,7 +139,7 @@
         )
         return c
 
-    lax.fori_loop(1, N, greet, 0)
+    lax.fori_loop(1, N, greet, 0, unroll=8)
 
     def exchange(which, src, dst, rows, pitch, src_block=None):
         def source(d):
@@ -146,7 +158,7 @@
             ).start()
             return c
 
-        lax.fori_loop(1, N, send, 0)
+        lax.fori_loop(1, N, send, 0, unroll=4)
         pltpu.make_async_copy(
             source(me), dst.at[pl.ds(me * pitch, rows), :], recv_sem.at[which]
         ).start()
@@ -159,10 +171,11 @@
         most = dst.at[pl.ds(0, (N - 1) * rows), :]
         pltpu.make_async_copy(most, most, send_sem.at[which]).wait()
 
-    entries = gate_entries(angles_ref[...])
+    loads[0].wait()
+    entries = gate_entries(angles_ref[...], trig_ref)
     for kind in range(4):
         for part in range(2):
-            gate_ref[2 * kind + part, pl.ds(0, 22), :] = entries[kind][part]
+            gate_ref[2 * kind + part, :, :] = entries[kind][part]
 
     def entry(kind, part, qubit, size):
         row = gate_ref[2 * kind + part, pl.ds(qubit, 1), :]
@@ -171,6 +184,8 @@
 
     lane_re, lane_im = kron_matrix(entry, list(range(0, 7)), True)
     row_re, row_im = kron_matrix(entry, list(range(7, 15)), False)
+    for load in loads[1:]:
+        load.wait()
     field = jnp.concatenate(
         [state_ref[pl.ds(0, 256, stride=2), :], state_ref[pl.ds(1, 256, stride=2), :]], axis=1
     )
@@ -188,33 +203,59 @@
     for half in range(2):
         send_amp[pl.ds(half, 128, stride=4), :] = amp_re[half * 128 : (half + 1) * 128]
         send_amp[pl.ds(2 + half, 128, stride=4), :] = amp_im[half * 128 : (half + 1) * 128]
+
+    ahead = jnp.where(iota((512, 256), 0) < iota((512, 256), 1), 1.0, 0.0)
+    ahead = jnp.where(iota((512, 256), 0) >= 256, 1.0, ahead).astype(BF16)
+    seen_ref[...] = jnp.zeros((128, 256), BF16)
+
+    def owners(step, sub):
+        at = step * 8 + 2 * sub
+        row = jnp.concatenate(
+            [high_ref[pl.ds(at, 1), :], high_ref[pl.ds(at + 1, 1), :]], axis=1
+        )
+        return iota((128, 256), 0) == row
+
+    def rank(step, c):
+        seen = seen_ref[...]
+        rows, hits = [], []
+        for sub in range(4):
+            mine = owners(step, sub)
+            hot = jnp.where(mine, 1.0, 0.0).astype(BF16)
+            rows.append(jnp.concatenate([hot, seen], axis=1))
+            hits.append(mine)
+            seen = seen + hot
+        seen_ref[...] = seen
+        counts = dot(jnp.concatenate(rows, axis=0), ahead)
+        for sub in range(4):
+            ranks = jnp.sum(
+                jnp.where(hits[sub], counts[128 * sub : 128 * (sub + 1)], 0.0),
+                axis=0,
+                keepdims=True,
+            )
+            for half in range(2):
+                rank_ref[pl.ds(step * 8 + 2 * sub + half, 1), :] = ranks[
+                    :, half * 128 : (half + 1) * 128
+                ].astype(I32)
+        return c
+
+    lax.fori_loop(0, 8, rank, 0)
     pl.semaphore_wait(barrier, N - 1)
     exchange(0, send_amp, recv_amp, 4, 4)
 
-    carry_ref[...] = jnp.zeros((128, 256), F32)
     place_ref[...] = jnp.zeros((256, 256), F32)
-    before = jnp.where(iota((256, 256), 0) < iota((256, 256), 1), 1.0, 0.0).astype(BF16)
-    prefix = jnp.concatenate([before, jnp.ones((256, 256), BF16)], axis=1)
 
     def route(step, c):
         lhs_parts, hot_parts = [], []
-        carry = carry_ref[...]
         for sub in range(4):
             at = step * 8 + 2 * sub
-            owner = jnp.concatenate(
-                [high_ref[pl.ds(at, 1), :], high_ref[pl.ds(at + 1, 1), :]], axis=1
-            )
             low = jnp.concatenate(
                 [low_ref[pl.ds(at, 1), :], low_ref[pl.ds(at + 1, 1), :]], axis=1
             )
-            mine = iota((128, 256), 0) == owner
-            hot = jnp.where(mine, 1.0, 0.0).astype(BF16)
-            counts = dot(hot, prefix)
-            rank = jnp.sum(
-                jnp.where(mine, counts[:, :256] + carry, 0.0), axis=0, keepdims=True
-            ).astype(I32)
-            carry = carry + counts[:, 256:]
-            ranked = jnp.where(iota((256, 256), 0) == rank, 1.0, 0.0).astype(BF16)
+            ranks = jnp.concatenate(
+                [rank_ref[pl.ds(at, 1), :], rank_ref[pl.ds(at + 1, 1), :]], axis=1
+            )
+            mine = owners(step, sub)
+            ranked = jnp.where(iota((256, 256), 0) == ranks, 1.0, 0.0).astype(BF16)
             rank_hot[:, pl.ds(pl.multiple_of(step * 1024 + sub * 256, 256), 256)] = ranked
             hot_parts.append(ranked)
             low_part = (low & 255).astype(F32)
@@ -224,7 +265,6 @@
                     [jnp.where(mine, low_part, 0.0), jnp.where(mine, high_part, 0.0)], axis=0
                 ).astype(BF16)
             )
-        carry_ref[...] = carry
         place_ref[...] += lax.dot_general(
             jnp.concatenate(lhs_parts, axis=1),
             jnp.concatenate(hot_parts, axis=1),
@@ -295,35 +335,83 @@
         send_hst[pl.ds(2 * row + 1, 1), :] = norm_part
     exchange(3, send_hst, recv_hst, 2, 2, lambda d: (d // 16) * 2)
 
+    my_z, my_x, my_yc = me // 32, lax.rem(me // 8, 4), lax.rem(me, 8)
+
+    def far(j):
+        return 2 + 3 * j + 3 * (j // 2) + 2 * (j // 3)
+
+    def chunk_base(k):
+        z = lax.rem(my_z + far(k // 4), 4)
+        x = lax.rem(my_x + far(lax.rem(k, 4)), 4)
+        return z * 32 + x * 8
+
+    def wanted_of(k):
+        at = chunk_base(k) * 2
+        return jnp.concatenate([recv_req[pl.ds(at + r, 1), :] for r in range(16)], axis=1)
+
     arrived(1, recv_req, 2)
+
+    def prepare(k, c):
+        column = (wanted_of(k) >> 7) & 127
+        want_hot[:, pl.ds(pl.multiple_of(k * 2048, 2048), 2048)] = jnp.where(
+            iota((128, 2048), 0) == column, 1.0, 0.0
+        ).astype(BF16)
+        return c
+
+    lax.fori_loop(0, 16, prepare, 0)
+
     arrived(2, recv_wgt, 2)
     table = jnp.concatenate(
         [recv_wgt[pl.ds(half, 128, stride=2), :].T for half in range(2)], axis=0
     )
     table = jnp.concatenate(split(table), axis=1)
 
-    def answer(step, c):
-        wanted = []
-        for sub in range(16):
-            wanted.append(recv_req[pl.ds(step * 16 + sub, 1), :])
-        wanted = jnp.concatenate(wanted, axis=1)
-        hot = jnp.where(iota((128, 2048), 0) == (wanted >> 7) & 127, 1.0, 0.0).astype(BF16)
+    def answer(k):
+        hot = want_hot[:, pl.ds(pl.multiple_of(k * 2048, 2048), 2048)]
         found = dot(table, jnp.concatenate([hot, hot], axis=0))
+        wanted = wanted_of(k)
         found = select_rows(found, [bit_of(wanted, p) for p in (14, 6, 5, 4, 3)])
         found = pick_sublane(found, wanted & 7)
-        for sub in range(16):
-            at = (step * 8 + sub // 2) * 4 + sub % 2
-            send_ans[pl.ds(at, 1), :] = found[:, sub * 128 : (sub + 1) * 128]
+        at = chunk_base(k) * 2
+        for r in range(16):
+            send_ans[pl.ds(at + r, 1), :] = found[:, r * 128 : (r + 1) * 128]
+
+    def reply(d):
+        pltpu.make_async_remote_copy(
+            src_ref=send_ans.at[pl.ds(d * 2, 2), :],
+            dst_ref=recv_ans.at[pl.ds(me * 2, 2), :],
+            send_sem=send_sem.at[4],
+            recv_sem=recv_sem.at[4],
+            device_id=(d,),
+            device_id_type=MESH,
+        ).start()
+
+    def reply_chunk(k):
+        base = chunk_base(k)
+        for j in range(8):
+            reply(base + j)
+
+    def two_chunks(step, c):
+        answer(2 * step)
+        answer(2 * step + 1)
+        reply_chunk(2 * step)
+        reply_chunk(2 * step + 1)
         return c
 
-    lax.fori_loop(0, 16, answer, 0)
-    fid_part = jnp.zeros((128, 128), F32)
-    for half in range(2):
-        valid = recv_req[pl.ds(half, 128, stride=2), :] >= 0
-        fid_part += jnp.where(valid, send_ans[pl.ds(half, 128, stride=4), :], 0.0)
-    fid_part = jnp.sum(fid_part, axis=0, keepdims=True)
-    send_ans[pl.ds(2, 128, stride=4), :] = jnp.broadcast_to(fid_part, (128, 128))
-    exchange(4, send_ans, recv_ans, 3, 4)
+    lax.fori_loop(0, 7, two_chunks, 0)
+    answer(14)
+    answer(15)
+    reply_chunk(14)
+    for j in range(1, 8):
+        reply(me - my_yc + lax.rem(my_yc + j, 8))
+    pltpu.make_async_copy(
+        send_ans.at[pl.ds(me * 2, 2), :], recv_ans.at[pl.ds(me * 2, 2), :], recv_sem.at[4]
+    ).start()
+    fid_part = jnp.sum(
+        jnp.where(recv_req[...] >= 0, send_ans[...], 0.0), axis=0, keepdims=True
+    )
+    send_fid[...] = jnp.broadcast_to(fid_part, (8, 128))
+    exchange(5, send_fid, recv_fid, 1, 1, lambda d: 0)
 
     arrived(3, recv_hst, 2)
     norm = jnp.sum(
@@ -334,16 +422,12 @@
     bins_row = pltpu.roll(bins_row, lax.rem(128 - lax.rem(me, 16) * 8, 128), 1)
     hist_ref[...] = bins_row[:, :8]
 
-    arrived(4, recv_ans, 3)
+    scale = 4194304.0 / norm
+    arrived(4, recv_ans, 2)
     answers = jnp.concatenate(
-        [recv_ans[pl.ds(half, 128, stride=4), :] for half in range(2)], axis=1
+        [recv_ans[pl.ds(half, 128, stride=2), :] for half in range(2)], axis=1
     )
     answers = jnp.concatenate(split(answers), axis=0)
-    total = jnp.sum(
-        jnp.sum(recv_ans[pl.ds(2, 128, stride=4), :], axis=0, keepdims=True), axis=1, keepdims=True
-    )
-    fid_ref[...] = 4194304.0 * (total / norm) / 1048576.0 - 1.0
-    scale = 4194304.0 / norm
 
     def collect(step, c):
         owner = jnp.concatenate([high_ref[pl.ds(step * 8 + k, 1), :] for k in range(8)], axis=1)
@@ -357,11 +441,18 @@
         return c
 
     lax.fori_loop(0, 8, collect, 0)
+
+    arrived(5, recv_fid, 1)
+    total = jnp.sum(
+        jnp.sum(recv_fid[...], axis=0, keepdims=True), axis=1, keepdims=True
+    )
+    fid_ref[...] = 4194304.0 * (total / norm) / 1048576.0 - 1.0
     sent(0, send_amp, 4)
     sent(1, send_req, 2)
     sent(2, send_wgt, 2)
     sent(3, recv_hst, 2)
-    sent(4, send_ans, 3)
+    sent(4, send_ans, 2)
+    sent(5, recv_fid, 1)
 
 
 def on_device(state, angles, sample_high, sample_low, marginal_qubits):
@@ -374,9 +465,15 @@
             jax.ShapeDtypeStruct((1, 8), F32),
             jax.ShapeDtypeStruct((1, 1), F32),
         ),
-        in_specs=[vmem, vmem, vmem, vmem, pl.BlockSpec(memory_space=pltpu.SMEM)],
+        in_specs=[pl.BlockSpec(memory_space=pl.ANY)] * 5,
         out_specs=(vmem, vmem, vmem),
         scratch_shapes=[
+            pltpu.VMEM((512, 128), F32),
+            pltpu.VMEM((3, 22), F32),
+            pltpu.VMEM((64, 128), I32),
+            pltpu.VMEM((64, 128), I32),
+            pltpu.SMEM((10,), I32),
+            pltpu.VMEM((8, 128), F32),
             pltpu.VMEM((8, 24, 128), F32),
             pltpu.VMEM((512, 128), F32),
             pltpu.VMEM((512, 128), F32),
@@ -386,18 +483,23 @@
             pltpu.VMEM((256, 128), F32),
             pltpu.VMEM((16, 128), F32),
             pltpu.VMEM((256, 128), F32),
-            pltpu.VMEM((512, 128), F32),
-            pltpu.VMEM((512, 128), F32),
+            pltpu.VMEM((256, 128), F32),
+            pltpu.VMEM((256, 128), F32),
+            pltpu.VMEM((8, 128), F32),
+            pltpu.VMEM((128, 128), F32),
             pltpu.VMEM((256, 8192), BF16),
-            pltpu.VMEM((128, 256), F32),
+            pltpu.VMEM((64, 128), I32),
+            pltpu.VMEM((128, 256), BF16),
             pltpu.VMEM((256, 256), F32),
-            pltpu.SemaphoreType.DMA((5,)),
+            pltpu.VMEM((128, 32768), BF16),
+            pltpu.SemaphoreType.DMA((6,)),
+            pltpu.SemaphoreType.DMA((6,)),
             pltpu.SemaphoreType.DMA((5,)),
         ],
         compiler_params=pltpu.CompilerParams(collective_id=0, has_side_effects=True),
     )(
         field,
-        angles,
+        angles.T,
         sample_high.reshape(64, 128),
         sample_low.reshape(64, 128),
         marginal_qubits,

time: 52.4 us -> 44.4 us (0.85)
  Pallas kernels: 46.6 us -> 39.9 us
  local copies, waits for them, and re-layouts: 3.25 us -> 1.89 us
    pallas_call x1, Pallas kernels: 46.6 us -> 39.9 us  [on_device(): pl.pallas_call(kernel, out_shape=(jax.ShapeDtypeStruct((64, 128), F32), j...]
    unnamed x7 -> x4, local copies, waits for them, and re-layouts: 3.25 us -> 1.89 us
where the time goes in v2:
time: 44.4 us; the launch traced here: 44.2 us
  Pallas kernels  39.9 us (90%)
  between operations  2.4 us (5%)
  local copies, waits for them, and re-layouts  1.89 us (4%)
    pallas_call x1, Pallas kernels, on_device(): pl.pallas_call(kernel, out_shape=(jax.ShapeDtypeStruct((64, 128), F32), j...  39.9 us
    unnamed x4, local copies, waits for them, and re-layouts  1.89 us

profile of v2, /device:TPU:1, one launch (start us, length us, event | category | flops | bytes accessed | tf_op | source)
XLA Modules:
  0.0 44.2 jit_solution(14711982267232666680)
XLA Ops:
  0.6 39.9 %shard_map.76 = (f32[64,128]{1,0:T(8,128)}, f32[1,8]{1,0:T(1,128)}, f32[1,1]{1,0:T(1,128)}) custom-call(f32[512,128]{1,0:T(8,128)} %bitcast.11, f32[3,22]{1,0:T(4,128)} %bitcast.15, s32[64,128]{1,0:T(8,128)} %bitcast.12, s32[64,128]{1,0:T(8,128)} %bitcast.13, s32[10]{0:T(128)} %marg_hbm.1), custom_call_target="tpu_custom_call" | custom-call | tf_op jit(solution)/shard_map/pallas_call | solution.py:461
  40.5 0.0 copy-start
  40.6 1.4 %copy.12 = f32[8192]{0:T(1024)} copy(f32[8192]{0:T(1024)} %bitcast.14) | data formatting | bytes 65536
  41.9 0.0 copy-done
  41.9 0.5 %copy.13 = f32[8]{0:T(128)} copy(f32[8]{0:T(128)S(1)} %bitcast.16) | data formatting | bytes 64
Async XLA Ops:
  40.5 1.4 %copy-start = (f32[1,8]{1,0:T(1,128)S(1)}, f32[1,8]{1,0:T(1,128)}, u32[]{:S(2)}) copy-start(f32[1,8]{1,0:T(1,128)} %get-tuple-element.7) | copy-start | bytes 100

commit v3 on v2

--- a/solution.py
+++ b/solution.py
@@ -104,6 +104,11 @@
     return jnp.sum(jnp.where(hit, values, 0.0), axis=0, keepdims=True)
 
 
+def one_hot(ids, rows):
+    one, zero = jnp.ones(ids.shape, BF16), jnp.zeros(ids.shape, BF16)
+    return jnp.concatenate([jnp.where(ids == row, one, zero) for row in rows], axis=1)
+
+
 def bit_of(x, place):
     return (x >> place) & 1 == 1
 
@@ -113,7 +118,7 @@
     probs_ref, hist_ref, fid_ref,
     state_ref, angles_ref, high_ref, low_ref, marg_ref, trig_ref, gate_ref, send_amp, recv_amp, send_req, recv_req, send_wgt, recv_wgt,
     send_hst, recv_hst, send_ans, recv_ans, send_fid, recv_fid,
-    rank_hot, rank_ref, seen_ref, place_ref, want_hot,
+    rank_hot, rank_ref, seen_ref, place_ref, want_hot, ids_ref,
     send_sem, recv_sem, load_sem,
 ):
     me = lax.axis_index("dev")
@@ -129,25 +134,45 @@
             ]
         )
     ]
+    my_z, my_x = me // 32, lax.rem(me // 8, 4)
+    my_y, my_core = lax.rem(me // 2, 4), lax.rem(me, 2)
+
+    def far(j):
+        return 2 + 3 * j + 3 * (j // 2) + 2 * (j // 3)
+
+    def chunk_base(k):
+        z = lax.rem(my_z + far(k // 4), 4)
+        x = lax.rem(my_x + far(lax.rem(k, 4)), 4)
+        return z * 32 + x * 8
+
+    inner = [lax.rem(my_y + far(j // 2), 4) * 2 + lax.rem(my_core + 1 + j, 2) for j in range(8)]
+
+    def others(act):
+        def chunk(k, c):
+            base = chunk_base(k)
+            for j in range(8):
+                act(base + inner[j])
+            return c
+
+        lax.fori_loop(0, 15, chunk, 0)
+        base = my_z * 32 + my_x * 8
+        for j in range(7):
+            act(base + inner[j])
+
+    barrier = pltpu.get_barrier_semaphore()
+
+    others(
+        lambda d: pl.semaphore_signal(barrier, inc=1, device_id=(d,), device_id_type=MESH)
+    )
     for load in loads:
         load.start()
-    barrier = pltpu.get_barrier_semaphore()
-
-    def greet(k, c):
-        pl.semaphore_signal(
-            barrier, inc=1, device_id=(lax.rem(me + k, N),), device_id_type=MESH
-        )
-        return c
-
-    lax.fori_loop(1, N, greet, 0, unroll=8)
 
     def exchange(which, src, dst, rows, pitch, src_block=None):
         def source(d):
             start = d * pitch if src_block is None else src_block(d)
             return src.at[pl.ds(start, rows), :]
 
-        def send(k, c):
-            d = lax.rem(me + k, N)
+        def send(d):
             pltpu.make_async_remote_copy(
                 src_ref=source(d),
                 dst_ref=dst.at[pl.ds(me * pitch, rows), :],
@@ -156,9 +181,8 @@
                 device_id=(d,),
                 device_id_type=MESH,
             ).start()
-            return c
-
-        lax.fori_loop(1, N, send, 0, unroll=4)
+
+        others(send)
         pltpu.make_async_copy(
             source(me), dst.at[pl.ds(me * pitch, rows), :], recv_sem.at[which]
         ).start()
@@ -171,6 +195,7 @@
         most = dst.at[pl.ds(0, (N - 1) * rows), :]
         pltpu.make_async_copy(most, most, send_sem.at[which]).wait()
 
+    ids_ref[...] = iota((256, 128), 0).astype(F32).astype(BF16)
     loads[0].wait()
     entries = gate_entries(angles_ref[...], trig_ref)
     for kind in range(4):
@@ -208,19 +233,14 @@
     ahead = jnp.where(iota((512, 256), 0) >= 256, 1.0, ahead).astype(BF16)
     seen_ref[...] = jnp.zeros((128, 256), BF16)
 
-    def owners(step, sub):
-        at = step * 8 + 2 * sub
-        row = jnp.concatenate(
-            [high_ref[pl.ds(at, 1), :], high_ref[pl.ds(at + 1, 1), :]], axis=1
-        )
-        return iota((128, 256), 0) == row
-
     def rank(step, c):
         seen = seen_ref[...]
         rows, hits = [], []
         for sub in range(4):
-            mine = owners(step, sub)
-            hot = jnp.where(mine, 1.0, 0.0).astype(BF16)
+            at = step * 8 + 2 * sub
+            owner = [high_ref[pl.ds(at + half, 1), :] for half in range(2)]
+            hot = one_hot(ids_ref[pl.ds(0, 128), :], [x.astype(F32).astype(BF16) for x in owner])
+            mine = iota((128, 256), 0) == jnp.concatenate(owner, axis=1)
             rows.append(jnp.concatenate([hot, seen], axis=1))
             hits.append(mine)
             seen = seen + hot
@@ -235,10 +255,10 @@
             for half in range(2):
                 rank_ref[pl.ds(step * 8 + 2 * sub + half, 1), :] = ranks[
                     :, half * 128 : (half + 1) * 128
-                ].astype(I32)
+                ]
         return c
 
-    lax.fori_loop(0, 8, rank, 0)
+    lax.fori_loop(0, 8, rank, 0, unroll=4)
     pl.semaphore_wait(barrier, N - 1)
     exchange(0, send_amp, recv_amp, 4, 4)
 
@@ -246,24 +266,21 @@
 
     def route(step, c):
         lhs_parts, hot_parts = [], []
-        for sub in range(4):
-            at = step * 8 + 2 * sub
-            low = jnp.concatenate(
-                [low_ref[pl.ds(at, 1), :], low_ref[pl.ds(at + 1, 1), :]], axis=1
-            )
-            ranks = jnp.concatenate(
-                [rank_ref[pl.ds(at, 1), :], rank_ref[pl.ds(at + 1, 1), :]], axis=1
-            )
-            mine = owners(step, sub)
-            ranked = jnp.where(iota((256, 256), 0) == ranks, 1.0, 0.0).astype(BF16)
-            rank_hot[:, pl.ds(pl.multiple_of(step * 1024 + sub * 256, 256), 256)] = ranked
+        ids = ids_ref[...]
+        none = jnp.zeros((128, 128), BF16)
+        for sub in range(8):
+            at = step * 8 + sub
+            low = low_ref[pl.ds(at, 1), :]
+            low_part = (low & 255).astype(F32).astype(BF16)
+            high_part = ((low >> 8) + 1).astype(F32).astype(BF16)
+            mine = ids[:128] == high_ref[pl.ds(at, 1), :].astype(F32).astype(BF16)
+            ranked = one_hot(ids, [rank_ref[pl.ds(at, 1), :].astype(BF16)])
+            rank_hot[:, pl.ds(pl.multiple_of(step * 1024 + sub * 128, 128), 128)] = ranked
             hot_parts.append(ranked)
-            low_part = (low & 255).astype(F32)
-            high_part = ((low >> 8) + 1).astype(F32)
             lhs_parts.append(
                 jnp.concatenate(
-                    [jnp.where(mine, low_part, 0.0), jnp.where(mine, high_part, 0.0)], axis=0
-                ).astype(BF16)
+                    [jnp.where(mine, low_part, none), jnp.where(mine, high_part, none)], axis=0
+                )
             )
         place_ref[...] += lax.dot_general(
             jnp.concatenate(lhs_parts, axis=1),
@@ -273,7 +290,7 @@
         )
         return c
 
-    lax.fori_loop(0, 8, route, 0)
+    lax.fori_loop(0, 8, route, 0, unroll=2)
     asked = (place_ref[:128, :] + 256.0 * (place_ref[128:, :] - 1.0)).astype(I32)
     for half in range(2):
         send_req[pl.ds(half, 128, stride=2), :] = asked[:, half * 128 : (half + 1) * 128]
@@ -335,16 +352,6 @@
         send_hst[pl.ds(2 * row + 1, 1), :] = norm_part
     exchange(3, send_hst, recv_hst, 2, 2, lambda d: (d // 16) * 2)
 
-    my_z, my_x, my_yc = me // 32, lax.rem(me // 8, 4), lax.rem(me, 8)
-
-    def far(j):
-        return 2 + 3 * j + 3 * (j // 2) + 2 * (j // 3)
-
-    def chunk_base(k):
-        z = lax.rem(my_z + far(k // 4), 4)
-        x = lax.rem(my_x + far(lax.rem(k, 4)), 4)
-        return z * 32 + x * 8
-
     def wanted_of(k):
         at = chunk_base(k) * 2
         return jnp.concatenate([recv_req[pl.ds(at + r, 1), :] for r in range(16)], axis=1)
@@ -352,10 +359,14 @@
     arrived(1, recv_req, 2)
 
     def prepare(k, c):
-        column = (wanted_of(k) >> 7) & 127
-        want_hot[:, pl.ds(pl.multiple_of(k * 2048, 2048), 2048)] = jnp.where(
-            iota((128, 2048), 0) == column, 1.0, 0.0
-        ).astype(BF16)
+        at = chunk_base(k) * 2
+        rows = [
+            ((recv_req[pl.ds(at + r, 1), :] >> 7) & 127).astype(F32).astype(BF16)
+            for r in range(16)
+        ]
+        want_hot[:, pl.ds(pl.multiple_of(k * 2048, 2048), 2048)] = one_hot(
+            ids_ref[pl.ds(0, 128), :], rows
+        )
         return c
 
     lax.fori_loop(0, 16, prepare, 0)
@@ -386,24 +397,12 @@
             device_id_type=MESH,
         ).start()
 
-    def reply_chunk(k):
-        base = chunk_base(k)
-        for j in range(8):
-            reply(base + j)
-
-    def two_chunks(step, c):
-        answer(2 * step)
-        answer(2 * step + 1)
-        reply_chunk(2 * step)
-        reply_chunk(2 * step + 1)
-        return c
-
-    lax.fori_loop(0, 7, two_chunks, 0)
-    answer(14)
-    answer(15)
-    reply_chunk(14)
-    for j in range(1, 8):
-        reply(me - my_yc + lax.rem(my_yc + j, 8))
+    for group in (range(0, 5), range(5, 10), range(10, 14), range(14, 16)):
+        for k in group:
+            answer(k)
+        for k in group:
+            for j in range(8 if k < 15 else 7):
+                reply(chunk_base(k) + inner[j])
     pltpu.make_async_copy(
         send_ans.at[pl.ds(me * 2, 2), :], recv_ans.at[pl.ds(me * 2, 2), :], recv_sem.at[4]
     ).start()
@@ -440,7 +439,7 @@
             probs_ref[pl.ds(step * 8 + k, 1), :] = found[:, k * 128 : (k + 1) * 128]
         return c
 
-    lax.fori_loop(0, 8, collect, 0)
+    lax.fori_loop(0, 8, collect, 0, unroll=4)
 
     arrived(5, recv_fid, 1)
     total = jnp.sum(
@@ -488,10 +487,11 @@
             pltpu.VMEM((8, 128), F32),
             pltpu.VMEM((128, 128), F32),
             pltpu.VMEM((256, 8192), BF16),
-            pltpu.VMEM((64, 128), I32),
+            pltpu.VMEM((64, 128), F32),
             pltpu.VMEM((128, 256), BF16),
             pltpu.VMEM((256, 256), F32),
             pltpu.VMEM((128, 32768), BF16),
+            pltpu.VMEM((256, 128), BF16),
             pltpu.SemaphoreType.DMA((6,)),
             pltpu.SemaphoreType.DMA((6,)),
             pltpu.SemaphoreType.DMA((5,)),

time: 44.4 us -> 42.3 us (0.953)
  Pallas kernels: 39.9 us -> 37.8 us
    pallas_call x1, Pallas kernels: 39.9 us -> 37.8 us  [on_device(): pl.pallas_call(kernel, out_shape=(jax.ShapeDtypeStruct((64, 128), F32), j...]
where the time goes in v3:
time: 42.3 us; the launch traced here: 42 us
  Pallas kernels  37.8 us (89%)
  between operations  2.4 us (6%)
  local copies, waits for them, and re-layouts  1.89 us (4%)
    pallas_call x1, Pallas kernels, on_device(): pl.pallas_call(kernel, out_shape=(jax.ShapeDtypeStruct((64, 128), F32), j...  37.8 us
    unnamed x4, local copies, waits for them, and re-layouts  1.89 us

profile of v3, /device:TPU:1, one launch (start us, length us, event | category | flops | bytes accessed | tf_op | source)
XLA Modules:
  0.0 42.0 jit_solution(14139924087783192505)
XLA Ops:
  0.6 37.8 %shard_map.76 = (f32[64,128]{1,0:T(8,128)}, f32[1,8]{1,0:T(1,128)}, f32[1,1]{1,0:T(1,128)}) custom-call(f32[512,128]{1,0:T(8,128)} %bitcast.11, f32[3,22]{1,0:T(4,128)} %bitcast.15, s32[64,128]{1,0:T(8,128)} %bitcast.12, s32[64,128]{1,0:T(8,128)} %bitcast.13, s32[10]{0:T(128)} %marg_hbm.1), custom_call_target="tpu_custom_call" | custom-call | tf_op jit(solution)/shard_map/pallas_call | solution.py:460
  38.4 0.0 copy-start
  38.4 1.4 %copy.12 = f32[8192]{0:T(1024)} copy(f32[8192]{0:T(1024)} %bitcast.14) | data formatting | bytes 65536
  39.8 0.0 copy-done
  39.8 0.5 %copy.13 = f32[8]{0:T(128)} copy(f32[8]{0:T(128)S(1)} %bitcast.16) | data formatting | bytes 64
Async XLA Ops:
  38.4 1.4 %copy-start = (f32[1,8]{1,0:T(1,128)S(1)}, f32[1,8]{1,0:T(1,128)}, u32[]{:S(2)}) copy-start(f32[1,8]{1,0:T(1,128)} %get-tuple-element.7) | copy-start | bytes 100

commit v4 on v3

--- a/solution.py
+++ b/solution.py
@@ -115,7 +115,7 @@
 
 def kernel(
     state_hbm, angles_hbm, high_hbm, low_hbm, marg_hbm,
-    probs_ref, hist_ref, fid_ref,
+    out_ref,
     state_ref, angles_ref, high_ref, low_ref, marg_ref, trig_ref, gate_ref, send_amp, recv_amp, send_req, recv_req, send_wgt, recv_wgt,
     send_hst, recv_hst, send_ans, recv_ans, send_fid, recv_fid,
     rank_hot, rank_ref, seen_ref, place_ref, want_hot, ids_ref,
@@ -134,38 +134,26 @@
             ]
         )
     ]
-    my_z, my_x = me // 32, lax.rem(me // 8, 4)
-    my_y, my_core = lax.rem(me // 2, 4), lax.rem(me, 2)
-
-    def far(j):
-        return 2 + 3 * j + 3 * (j // 2) + 2 * (j // 3)
-
-    def chunk_base(k):
-        z = lax.rem(my_z + far(k // 4), 4)
-        x = lax.rem(my_x + far(lax.rem(k, 4)), 4)
-        return z * 32 + x * 8
-
-    inner = [lax.rem(my_y + far(j // 2), 4) * 2 + lax.rem(my_core + 1 + j, 2) for j in range(8)]
+    my_z, my_x = me // 32, (me // 8) & 3
+    my_y, my_core = (me // 2) & 3, me & 1
+
+    ring = (2, 1, 3, 0)
+    z_part = [((my_z + off) & 3) * 32 for off in ring]
+    x_part = [((my_x + off) & 3) * 8 for off in ring]
+    inner = [((my_y + ring[j // 2]) & 3) * 2 + ((my_core + 1 + j) & 1) for j in range(8)]
+    bases = [z_part[k // 4] + x_part[k % 4] for k in range(16)]
 
     def others(act):
-        def chunk(k, c):
-            base = chunk_base(k)
-            for j in range(8):
-                act(base + inner[j])
-            return c
-
-        lax.fori_loop(0, 15, chunk, 0)
-        base = my_z * 32 + my_x * 8
-        for j in range(7):
-            act(base + inner[j])
-
+        for k in range(16):
+            for j in range(8 if k < 15 else 7):
+                act(bases[k] + inner[j])
+
+    for load in loads:
+        load.start()
     barrier = pltpu.get_barrier_semaphore()
-
     others(
         lambda d: pl.semaphore_signal(barrier, inc=1, device_id=(d,), device_id_type=MESH)
     )
-    for load in loads:
-        load.start()
 
     def exchange(which, src, dst, rows, pitch, src_block=None):
         def source(d):
@@ -353,23 +341,17 @@
     exchange(3, send_hst, recv_hst, 2, 2, lambda d: (d // 16) * 2)
 
     def wanted_of(k):
-        at = chunk_base(k) * 2
+        at = bases[k] * 2
         return jnp.concatenate([recv_req[pl.ds(at + r, 1), :] for r in range(16)], axis=1)
 
     arrived(1, recv_req, 2)
 
-    def prepare(k, c):
-        at = chunk_base(k) * 2
+    for k in range(16):
         rows = [
-            ((recv_req[pl.ds(at + r, 1), :] >> 7) & 127).astype(F32).astype(BF16)
+            ((recv_req[pl.ds(bases[k] * 2 + r, 1), :] >> 7) & 127).astype(F32).astype(BF16)
             for r in range(16)
         ]
-        want_hot[:, pl.ds(pl.multiple_of(k * 2048, 2048), 2048)] = one_hot(
-            ids_ref[pl.ds(0, 128), :], rows
-        )
-        return c
-
-    lax.fori_loop(0, 16, prepare, 0)
+        want_hot[:, pl.ds(k * 2048, 2048)] = one_hot(ids_ref[pl.ds(0, 128), :], rows)
 
     arrived(2, recv_wgt, 2)
     table = jnp.concatenate(
@@ -378,12 +360,12 @@
     table = jnp.concatenate(split(table), axis=1)
 
     def answer(k):
-        hot = want_hot[:, pl.ds(pl.multiple_of(k * 2048, 2048), 2048)]
+        hot = want_hot[:, pl.ds(k * 2048, 2048)]
         found = dot(table, jnp.concatenate([hot, hot], axis=0))
         wanted = wanted_of(k)
         found = select_rows(found, [bit_of(wanted, p) for p in (14, 6, 5, 4, 3)])
         found = pick_sublane(found, wanted & 7)
-        at = chunk_base(k) * 2
+        at = bases[k] * 2
         for r in range(16):
             send_ans[pl.ds(at + r, 1), :] = found[:, r * 128 : (r + 1) * 128]
 
@@ -402,7 +384,7 @@
             answer(k)
         for k in group:
             for j in range(8 if k < 15 else 7):
-                reply(chunk_base(k) + inner[j])
+                reply(bases[k] + inner[j])
     pltpu.make_async_copy(
         send_ans.at[pl.ds(me * 2, 2), :], recv_ans.at[pl.ds(me * 2, 2), :], recv_sem.at[4]
     ).start()
@@ -419,7 +401,7 @@
     bins_row = jnp.sum(recv_hst[pl.ds(0, 128, stride=2), :], axis=0, keepdims=True)
     bins_row = 1024.0 * (bins_row / norm)
     bins_row = pltpu.roll(bins_row, lax.rem(128 - lax.rem(me, 16) * 8, 128), 1)
-    hist_ref[...] = bins_row[:, :8]
+    out_ref[pl.ds(64, 1), :] = bins_row
 
     scale = 4194304.0 / norm
     arrived(4, recv_ans, 2)
@@ -436,7 +418,7 @@
         found = select_rows(found, [bit_of(owner, p) for p in (6, 5, 4, 3)])
         found = pick_sublane(found, owner & 7) * scale
         for k in range(8):
-            probs_ref[pl.ds(step * 8 + k, 1), :] = found[:, k * 128 : (k + 1) * 128]
+            out_ref[pl.ds(step * 8 + k, 1), :] = found[:, k * 128 : (k + 1) * 128]
         return c
 
     lax.fori_loop(0, 8, collect, 0, unroll=4)
@@ -445,7 +427,8 @@
     total = jnp.sum(
         jnp.sum(recv_fid[...], axis=0, keepdims=True), axis=1, keepdims=True
     )
-    fid_ref[...] = 4194304.0 * (total / norm) / 1048576.0 - 1.0
+    fidelity = 4194304.0 * (total / norm) / 1048576.0 - 1.0
+    out_ref[pl.ds(65, 1), :] = jnp.broadcast_to(fidelity, (1, 128))
     sent(0, send_amp, 4)
     sent(1, send_req, 2)
     sent(2, send_wgt, 2)
@@ -454,18 +437,20 @@
     sent(5, recv_fid, 1)
 
 
+def unpack(packed_ref, probs_ref, hist_ref, fid_ref):
+    probs_ref[...] = packed_ref[pl.ds(0, 64), :]
+    hist_ref[...] = packed_ref[pl.ds(64, 1), pl.ds(0, 8)]
+    fid_ref[...] = packed_ref[pl.ds(65, 1), pl.ds(0, 1)]
+
+
 def on_device(state, angles, sample_high, sample_low, marginal_qubits):
     vmem = pl.BlockSpec(memory_space=pltpu.VMEM)
     field = state.reshape(2, 256, 128).transpose(1, 0, 2).reshape(512, 128)
-    probs, hist, fid = pl.pallas_call(
+    packed = pl.pallas_call(
         kernel,
-        out_shape=(
-            jax.ShapeDtypeStruct((64, 128), F32),
-            jax.ShapeDtypeStruct((1, 8), F32),
-            jax.ShapeDtypeStruct((1, 1), F32),
-        ),
+        out_shape=jax.ShapeDtypeStruct((72, 128), F32),
         in_specs=[pl.BlockSpec(memory_space=pl.ANY)] * 5,
-        out_specs=(vmem, vmem, vmem),
+        out_specs=vmem,
         scratch_shapes=[
             pltpu.VMEM((512, 128), F32),
             pltpu.VMEM((3, 22), F32),
@@ -504,6 +489,16 @@
         sample_low.reshape(64, 128),
         marginal_qubits,
     )
+    probs, hist, fid = pl.pallas_call(
+        unpack,
+        out_shape=(
+            jax.ShapeDtypeStruct((64, 128), F32),
+            jax.ShapeDtypeStruct((1, 8), F32),
+            jax.ShapeDtypeStruct((1, 1), F32),
+        ),
+        in_specs=[vmem],
+        out_specs=(vmem, vmem, vmem),
+    )(packed)
     return probs.reshape(8192), hist.reshape(8), fid.reshape(())
 
 

time: 42.3 us -> 38.1 us (0.901)
  local copies, waits for them, and re-layouts: 1.89 us -> 0 us
  between operations: 2.4 us -> 0.64 us
  Pallas kernels: 37.8 us -> 37.3 us
    unnamed x4 -> x0, local copies, waits for them, and re-layouts: 1.89 us -> none
    pallas_call x1 -> x2, Pallas kernels: 37.8 us -> 37.3 us  [the longest x1 35.9 us: on_device(): pl.pallas_call(kernel, out_shape=jax.ShapeDtypeStruct((72, 128), F32), in...]
where the time goes in v4:
time: 38.1 us; the launch traced here: 38 us
  Pallas kernels  37.3 us (98%)
  between operations  0.64 us (2%)
    pallas_call x1, Pallas kernels, on_device(): pl.pallas_call(kernel, out_shape=jax.ShapeDtypeStruct((72, 128), F32), in...  35.9 us
    pallas_call x1, Pallas kernels, on_device(): pl.pallas_call(unpack, out_shape=(jax.ShapeDtypeStruct((64, 128), F32), j...  1.39 us

profile of v4, /device:TPU:1, one launch (start us, length us, event | category | flops | bytes accessed | tf_op | source)
XLA Modules:
  0.0 38.0 jit_solution(7213727445835029280)
XLA Ops:
  0.6 35.9 %shard_map.76.packed_ref = f32[72,128]{1,0:T(8,128)} custom-call(f32[512,128]{1,0:T(8,128)} %bitcast.11, f32[3,22]{1,0:T(4,128)} %bitcast.14, s32[64,128]{1,0:T(8,128)} %bitcast.12, s32[64,128]{1,0:T(8,128)} %bitcast.13, s32[10]{0:T(128)} %marg_hbm.1), custom_call_target="tpu_custom_call" | custom-call | tf_op jit(solution)/shard_map/pallas_call | solution.py:449
  36.6 1.4 %shard_map.77 = (f32[64,128]{1,0:T(8,128)}, f32[1,8]{1,0:T(1,128)}, f32[1,1]{1,0:T(1,128)}) custom-call(f32[72,128]{1,0:T(8,128)} %shard_map.76.packed_ref), custom_call_target="tpu_custom_call" | custom-call | tf_op jit(solution)/shard_map/pallas_call | solution.py:492

commit v5 on v4

--- a/solution.py
+++ b/solution.py
@@ -379,7 +379,7 @@
             device_id_type=MESH,
         ).start()
 
-    for group in (range(0, 5), range(5, 10), range(10, 14), range(14, 16)):
+    for group in (range(0,6),range(6,12),range(12,15),range(15,16)):
         for k in group:
             answer(k)
         for k in group:
@@ -446,6 +446,13 @@
 def on_device(state, angles, sample_high, sample_low, marginal_qubits):
     vmem = pl.BlockSpec(memory_space=pltpu.VMEM)
     field = state.reshape(2, 256, 128).transpose(1, 0, 2).reshape(512, 128)
+    operands = (
+        field,
+        angles.T,
+        sample_high.reshape(64, 128),
+        sample_low.reshape(64, 128),
+        marginal_qubits,
+    )
     packed = pl.pallas_call(
         kernel,
         out_shape=jax.ShapeDtypeStruct((72, 128), F32),
@@ -481,14 +488,10 @@
             pltpu.SemaphoreType.DMA((6,)),
             pltpu.SemaphoreType.DMA((5,)),
         ],
-        compiler_params=pltpu.CompilerParams(collective_id=0, has_side_effects=True),
-    )(
-        field,
-        angles.T,
-        sample_high.reshape(64, 128),
-        sample_low.reshape(64, 128),
-        marginal_qubits,
-    )
+        compiler_params=pltpu.CompilerParams(
+            collective_id=0, has_side_effects=True, vmem_limit_bytes=40 * 1024 * 1024
+        ),
+    )(*(pltpu.with_memory_space_constraint(x, pltpu.HBM) for x in operands))
     probs, hist, fid = pl.pallas_call(
         unpack,
         out_shape=(
@@ -498,6 +501,7 @@
         ),
         in_specs=[vmem],
         out_specs=(vmem, vmem, vmem),
+        compiler_params=pltpu.CompilerParams(vmem_limit_bytes=8 * 1024 * 1024),
     )(packed)
     return probs.reshape(8192), hist.reshape(8), fid.reshape(())
 

time: 38.1 us -> 36.6 us (0.961)
  Pallas kernels: 37.3 us -> 35.8 us
    pallas_call x1, Pallas kernels: 1.39 us -> 0.62 us  [on_device(): pl.pallas_call(unpack, out_shape=(jax.ShapeDtypeStruct((64, 128), F32), j...]
    pallas_call x1, Pallas kernels: 35.9 us -> 35.2 us  [on_device(): pl.pallas_call(kernel, out_shape=jax.ShapeDtypeStruct((72, 128), F32), in...]
where the time goes in v5:
time: 36.6 us; the launch traced here: 36.5 us
  Pallas kernels  35.8 us (98%)
  between operations  0.64 us (2%)
    pallas_call x1, Pallas kernels, on_device(): pl.pallas_call(kernel, out_shape=jax.ShapeDtypeStruct((72, 128), F32), in...  35.2 us

profile of v5, /device:TPU:1, one launch (start us, length us, event | category | flops | bytes accessed | tf_op | source)
XLA Modules:
  0.0 36.5 jit_solution(6792839831300580326)
XLA Ops:
  0.6 35.2 %shard_map.76.packed_ref = f32[72,128]{1,0:T(8,128)S(1)} custom-call(f32[512,128]{1,0:T(8,128)} %bitcast.11, f32[3,22]{1,0:T(4,128)} %bitcast.14, s32[64,128]{1,0:T(8,128)} %bitcast.12, s32[64,128]{1,0:T(8,128)} %bitcast.13, s32[10]{0:T(128)} %marg_hbm.1), custom_call_target="tpu_custom_call" | custom-call | tf_op jit(solution)/shard_map/pallas_call | solution.py:456
  35.8 0.6 %shard_map.77 = (f32[64,128]{1,0:T(8,128)}, f32[1,8]{1,0:T(1,128)}, f32[1,1]{1,0:T(1,128)}) custom-call(f32[72,128]{1,0:T(8,128)S(1)} %shard_map.76.packed_ref), custom_call_target="tpu_custom_call" | custom-call | tf_op jit(solution)/shard_map/pallas_call | solution.py:495

commit v6 on v5

--- a/solution.py
+++ b/solution.py
@@ -379,7 +379,7 @@
             device_id_type=MESH,
         ).start()
 
-    for group in (range(0,6),range(6,12),range(12,15),range(15,16)):
+    for group in (range(0, 5), range(5, 9), range(9, 12), range(12, 14), range(14, 15), range(15, 16)):
         for k in group:
             answer(k)
         for k in group:
@@ -421,7 +421,7 @@
             out_ref[pl.ds(step * 8 + k, 1), :] = found[:, k * 128 : (k + 1) * 128]
         return c
 
-    lax.fori_loop(0, 8, collect, 0, unroll=4)
+    lax.fori_loop(0, 8, collect, 0, unroll=8)
 
     arrived(5, recv_fid, 1)
     total = jnp.sum(
@@ -437,10 +437,12 @@
     sent(5, recv_fid, 1)
 
 
-def unpack(packed_ref, probs_ref, hist_ref, fid_ref):
-    probs_ref[...] = packed_ref[pl.ds(0, 64), :]
+def unpack(packed_ref, probs_hbm, hist_ref, fid_ref, sem):
+    probs = pltpu.make_async_copy(packed_ref.at[pl.ds(0, 64), :], probs_hbm, sem)
+    probs.start()
     hist_ref[...] = packed_ref[pl.ds(64, 1), pl.ds(0, 8)]
     fid_ref[...] = packed_ref[pl.ds(65, 1), pl.ds(0, 1)]
+    probs.wait()
 
 
 def on_device(state, angles, sample_high, sample_low, marginal_qubits):
@@ -500,7 +502,8 @@
             jax.ShapeDtypeStruct((1, 1), F32),
         ),
         in_specs=[vmem],
-        out_specs=(vmem, vmem, vmem),
+        out_specs=(pl.BlockSpec(memory_space=pl.ANY), vmem, vmem),
+        scratch_shapes=[pltpu.SemaphoreType.DMA],
         compiler_params=pltpu.CompilerParams(vmem_limit_bytes=8 * 1024 * 1024),
     )(packed)
     return probs.reshape(8192), hist.reshape(8), fid.reshape(())

time: 36.6 us -> 37.2 us (1.016)
  Pallas kernels: 35.8 us -> 36.3 us
    pallas_call x1, Pallas kernels: 0.62 us -> 1.14 us  [on_device(): pl.pallas_call(unpack, out_shape=(jax.ShapeDtypeStruct((64, 128), F32), j...]
where the time goes in v6:
time: 37.2 us; the launch traced here: 37.1 us
  Pallas kernels  36.3 us (98%)
  between operations  0.8 us (2%)
    pallas_call x1, Pallas kernels, on_device(): pl.pallas_call(kernel, out_shape=jax.ShapeDtypeStruct((72, 128), F32), in...  35.2 us
    pallas_call x1, Pallas kernels, on_device(): pl.pallas_call(unpack, out_shape=(jax.ShapeDtypeStruct((64, 128), F32), j...  1.14 us

profile of v6, /device:TPU:1, one launch (start us, length us, event | category | flops | bytes accessed | tf_op | source)
XLA Modules:
  0.0 37.1 jit_solution(16834823061562805781)
XLA Ops:
  0.6 35.2 %shard_map.76.packed_ref = f32[72,128]{1,0:T(8,128)S(1)} custom-call(f32[512,128]{1,0:T(8,128)} %bitcast.11, f32[3,22]{1,0:T(4,128)} %bitcast.14, s32[64,128]{1,0:T(8,128)} %bitcast.12, s32[64,128]{1,0:T(8,128)} %bitcast.13, s32[10]{0:T(128)} %marg_hbm.1), custom_call_target="tpu_custom_call" | custom-call | tf_op jit(solution)/shard_map/pallas_call | solution.py:458
  35.8 1.1 %shard_map.77 = (f32[64,128]{1,0:T(8,128)}, f32[1,8]{1,0:T(1,128)}, f32[1,1]{1,0:T(1,128)}) custom-call(f32[72,128]{1,0:T(8,128)S(1)} %shard_map.76.packed_ref), custom_call_target="tpu_custom_call" | custom-call | tf_op jit(solution)/shard_map/pallas_call | solution.py:497

commit v7 on v5

--- a/solution.py
+++ b/solution.py
@@ -140,7 +140,7 @@
     ring = (2, 1, 3, 0)
     z_part = [((my_z + off) & 3) * 32 for off in ring]
     x_part = [((my_x + off) & 3) * 8 for off in ring]
-    inner = [((my_y + ring[j // 2]) & 3) * 2 + ((my_core + 1 + j) & 1) for j in range(8)]
+    inner = [((my_y + ring[j // 2]) & 3) * 2 + ((1 + j + my_core * (j // 6)) & 1) for j in range(8)]
     bases = [z_part[k // 4] + x_part[k % 4] for k in range(16)]
 
     def others(act):

time: 36.6 us -> 36.6 us (level)
  no operation moved by 1% of the time
where the time goes in v7:
time: 36.6 us; the launch traced here: 36.5 us
  Pallas kernels  35.9 us (98%)
  between operations  0.64 us (2%)
    pallas_call x1, Pallas kernels, on_device(): pl.pallas_call(kernel, out_shape=jax.ShapeDtypeStruct((72, 128), F32), in...  35.2 us

profile of v7, /device:TPU:1, one launch (start us, length us, event | category | flops | bytes accessed | tf_op | source)
XLA Modules:
  0.0 36.5 jit_solution(17949423783010455350)
XLA Ops:
  0.6 35.2 %shard_map.76.packed_ref = f32[72,128]{1,0:T(8,128)S(1)} custom-call(f32[512,128]{1,0:T(8,128)} %bitcast.11, f32[3,22]{1,0:T(4,128)} %bitcast.14, s32[64,128]{1,0:T(8,128)} %bitcast.12, s32[64,128]{1,0:T(8,128)} %bitcast.13, s32[10]{0:T(128)} %marg_hbm.1), custom_call_target="tpu_custom_call" | custom-call | tf_op jit(solution)/shard_map/pallas_call | solution.py:456
  35.9 0.6 %shard_map.77 = (f32[64,128]{1,0:T(8,128)}, f32[1,8]{1,0:T(1,128)}, f32[1,1]{1,0:T(1,128)}) custom-call(f32[72,128]{1,0:T(8,128)S(1)} %shard_map.76.packed_ref), custom_call_target="tpu_custom_call" | custom-call | tf_op jit(solution)/shard_map/pallas_call | solution.py:495
